TPU v7x, 32 devices: a whole 2x2x4 slice. The times are simulated.
32 devices in a mesh: feat: 4 (over y, x), dp: 8 (over z, core).
Axes of the slice: x: 2, y: 2, z: 4, core: 2. Of those that a mesh axis runs over, the one named last changes fastest.
Arguments:
- layer_inputs: bfloat16 [4, 24, 128, 5120], P('feat', 'dp'), may hold values from -6 to 6
- output_grads: bfloat16 [4, 24, 128, 5120], P('feat', 'dp'), may hold values from -6 to 6
- adapter_a: bfloat16 [4, 128, 5120], P('feat'), may hold values from -0.078125 to 0.078125
- adapter_b: bfloat16 [4, 5120, 128], P('feat'), may hold values from -0.5 to 0.5
- out_factor: bfloat16 [4, 5120, 64], P('feat'), may hold values from -0.5 to 0.5
- in_factor: bfloat16 [4, 5120, 64], P('feat'), may hold values from -0.5 to 0.5
- rank_factor_b: bfloat16 [4, 128, 128], P('feat'), may hold values from -0.5 to 0.5
- rank_factor_a: bfloat16 [4, 128, 128], P('feat'), may hold values from -0.5 to 0.5
- token_counts: int32 [24], P('dp'), may hold values from 16 to 128, as said below
- val_grads: bfloat16 [256, 8192], P('dp', 'feat'), may hold values from -40 to 40
- val_domain: int32 [256, 1], P('dp'), may hold values from 0 to 7
Outputs:
- train_features: bfloat16 [24, 8192], P('dp', 'feat')
- domain_scores: float32 [24, 8], P('dp')
Inputs may be any that keep to these rules, and one draw needn't show every extreme that they name: `token_counts`: some example has all 128 positions live; positions at or past an example's count are padding.
All inputs are finite; a program needn't handle non-finite values.
Results may differ from a plain program's by a relative error of at most 0.0064.
Values may be sent and summed in bfloat16 or wider, within the bound.
No kernel may reach another device: no remote copies, remote signals or barrier semaphores. Data moves between devices by JAX's collectives and lax.ppermute only.
A program may use at most 64 MiB of HBM per device.

v0:
```python
import math

import jax
import jax.numpy as jnp
from jax import lax
from jax.sharding import PartitionSpec as P

PROJ = 8192
DOMAINS = 8


norm_eps = 1e-06


def contract_last(left_side, right_side):
    return lax.dot_general(
        left_side, right_side, (((1,), (1,)), ((), ())), preferred_element_type=jnp.float32
    )


def local(
    layer_inputs,
    output_grads,
    adapter_a,
    adapter_b,
    out_factor,
    in_factor,
    rank_factor_b,
    rank_factor_a,
    token_counts,
    val_grads,
    val_domain,
):
    local_count, examples, seq_len, width = layer_inputs.shape
    rank = adapter_a.shape[1]
    rows_proj = out_factor.shape[2]
    cols_proj = rank_factor_b.shape[2]
    positions = lax.broadcasted_iota(jnp.int32, (examples, seq_len), 1)
    live_mask = positions < token_counts[:, None]
    both_mask = jnp.concatenate([live_mask, live_mask], axis=1)[:, :, None]
    inputs_two = layer_inputs[0].reshape(examples * seq_len, width)
    grads_two = output_grads[0].reshape(examples * seq_len, width)
    input_weights = jnp.concatenate([adapter_a[0].T, in_factor[0]], axis=1)
    grad_weights = jnp.concatenate([adapter_b[0], out_factor[0]], axis=1)
    from_inputs = jnp.dot(inputs_two, input_weights, preferred_element_type=jnp.float32)
    from_grads = jnp.dot(grads_two, grad_weights, preferred_element_type=jnp.float32)
    hidden = from_inputs[:, :rank].astype(jnp.bfloat16)
    input_proj = from_inputs[:, rank:].astype(jnp.bfloat16)
    backward = from_grads[:, :rank].astype(jnp.bfloat16)
    grad_proj = from_grads[:, rank:].astype(jnp.bfloat16)
    hidden_rank = jnp.dot(hidden, rank_factor_b[0], preferred_element_type=jnp.float32).astype(
        jnp.bfloat16
    )
    back_rank = jnp.dot(backward, rank_factor_a[0], preferred_element_type=jnp.float32).astype(
        jnp.bfloat16
    )
    left_side = jnp.concatenate(
        [
            grad_proj.reshape(examples, seq_len, rows_proj),
            input_proj.reshape(examples, seq_len, rows_proj),
        ],
        axis=1,
    )
    right_side = jnp.concatenate(
        [
            hidden_rank.reshape(examples, seq_len, cols_proj),
            back_rank.reshape(examples, seq_len, cols_proj),
        ],
        axis=1,
    )
    left_side = jnp.where(both_mask, left_side, jnp.zeros_like(left_side))
    summed = jnp.einsum("etk,etj->ekj", left_side, right_side, preferred_element_type=jnp.float32)
    partial_terms = summed.reshape(examples, rows_proj * cols_proj)
    reduced = lax.psum_scatter(partial_terms, "feat", scatter_dimension=1, tiled=True)
    counts_float = token_counts.astype(jnp.float32)
    train_features = (reduced / counts_float[:, None]).astype(jnp.bfloat16)
    train_float = train_features.astype(jnp.float32)
    domain_ids = lax.broadcasted_iota(jnp.int32, (val_grads.shape[0], DOMAINS), 1)
    local_marks = (val_domain == domain_ids).astype(jnp.bfloat16)
    score_scale = math.sqrt(PROJ)
    shard_rows = lax.all_gather(val_grads, "dp", axis=0, tiled=True)
    shard_marks = lax.all_gather(local_marks, "dp", axis=0, tiled=True)
    inner_block = contract_last(train_features, shard_rows)
    shard_float = shard_rows.astype(jnp.float32)
    norm_block = jnp.sum(shard_float * shard_float, axis=1)
    domain_marks = shard_marks.astype(jnp.float32)
    train_part = jnp.sum(train_float * train_float, axis=1)
    inner_dots, train_norm, val_norm = lax.psum((inner_block, train_part, norm_block), "feat")
    cosine = (
        inner_dots
        * lax.rsqrt(train_norm + norm_eps)[:, None]
        * lax.rsqrt(val_norm + norm_eps)[None, :]
    )
    domain_sizes = jnp.sum(domain_marks, axis=0)
    totals = jnp.dot(cosine, domain_marks, precision=lax.Precision.HIGHEST)
    domain_scores = score_scale * totals / domain_sizes[None, :]
    return (train_features, domain_scores)


def solution(mesh):
    in_specs = (
        P("feat", "dp", None, None),
        P("feat", "dp", None, None),
        P("feat", None, None),
        P("feat", None, None),
        P("feat", None, None),
        P("feat", None, None),
        P("feat", None, None),
        P("feat", None, None),
        P("dp"),
        P("dp", "feat"),
        P("dp", None),
    )
    out_specs = (P("dp", "feat"), P("dp", None))
    return jax.shard_map(local, mesh=mesh, in_specs=in_specs, out_specs=out_specs, check_vma=False)
```

profile of v0, /device:TPU:0, one launch (start us, length us, event | category | flops | bytes accessed | tf_op | source)
XLA Modules:
  0.0 99.0 jit_solution(2255923739240428739)
XLA Ops:
  8.0 0.0 copy-start
  8.0 0.0 reduce-scatter.4.cloned.1.call-start
  8.1 1.7 %copy.20 = bf16[5120,64]{1,0:T(8,128)(2,1)S(1)} copy(bf16[5120,64]{0,1:T(8,128)(2,1)} %bitcast.40) | data formatting | bytes 1310720 | tf_op jit(solution)/shard_map/squeeze | solution.py:44
  9.7 0.0 copy-start.4
  9.7 0.0 copy-start.5
  9.7 4.4 %fusion.14 = bf16[384,192]{0,1:T(8,128)(2,1)S(1)} fusion(bf16[384,5120]{1,0:T(8,128)(2,1)} %bitcast.44, bf16[5120,64]{1,0:T(8,128)(2,1)S(1)} %copy.20, bf16[5120,128]{1,0:T(8,128)(2,1)} %bitcast.46), kind=kOutput, calls=%fused_computation.11 | convolution fusion | flops 758980608 | bytes 6045696 | tf_op jit(solution)/shard_map/dot_general | solution.py:46
  14.1 0.0 copy-done.4
  14.2 0.0 copy-done.5
  14.2 0.0 copy-start.6
  14.2 0.0 copy-start.2
  14.2 3.6 %fusion.17 = bf16[384,192]{0,1:T(8,128)(2,1)S(1)} fusion(bf16[384,5120]{1,0:T(8,128)(2,1)} %bitcast.45, bf16[5120,64]{0,1:T(8,128)(2,1)S(1)} %bitcast.48, bf16[5120,128]{0,1:T(8,128)(2,1)S(1)} %bitcast.47), kind=kOutput, calls=%fused_computation.12 | convolution fusion | flops 758980608 | bytes 6045696 | tf_op jit(solution)/shard_map/dot_general | solution.py:45
  17.8 0.0 copy-done.6
  17.8 0.1 iota_compare_fusion.1
  17.9 0.0 copy-done
  17.9 0.2 convolution_convert_fusion
  18.1 0.0 copy-done.2
  18.1 0.2 convolution_convert_fusion.1
  18.3 0.1 maximum_select_fusion
  18.4 0.2 fusion.21
  18.6 2.6 %copy.25 = f32[3,64,128]{0,2,1:T(8,128)} copy(f32[3,64,128]{2,1,0:T(8,128)S(1)} %fusion.21) | data formatting | bytes 196608
  21.2 0.0 copy-start.3
  21.2 0.0 reduce-scatter.4.cloned.1.call-update
  21.3 0.0 all-gather.3.cloned.1.call-start
  21.3 0.5 all-gather.3.cloned.1.call-update
  21.8 0.0 copy-done.3
  21.9 14.5 %all-gather = bf16[8,32,8]{1,2,0:T(8,128)(2,1)S(1)} all-gather(bf16[1,32,8]{1,2,0:T(8,128)(2,1)S(1)} %fusion.33), channel_id=1, replica_groups=mesh['feat'=4,'dp'=8] {'dp'}, dimensions={0}, use_global_device_ids=true | all-gather | bytes 4608 | tf_op jit(solution)/shard_map/all_gather | solution.py:82
  36.4 0.1 reshape.31
  36.4 0.1 convert_reduce_fusion
  36.6 40.2 %reduce-scatter.4.cloned.1.call-done = f32[2048,3]{1,0:T(8,128)} async-done(((f32[8192,3]{1,0:T(8,128)}), f32[2048,3]{1,0:T(8,128)}) %reduce-scatter.4.cloned.1.call-update) | async-done | bytes 24592
  76.7 1.6 %copy.24 = f32[3,2048]{1,0:T(4,128)S(1)} copy(f32[3,2048]{0,1:T(8,128)} %bitcast.39) | data formatting | bytes 49152
  78.3 0.2 multiply_reduce_fusion.1
  78.5 0.0 copy-start.1
  78.5 0.0 all-gather.3.cloned.1.call-done
  78.5 1.5 %multiply_reduce_fusion = f32[256]{0:T(256)S(1)} fusion(bf16[256,2048]{1,0:T(8,128)(2,1)} %all-gather.3.cloned.1.call-done), kind=kLoop, calls=%fused_computation.4 | loop fusion | flops 1572608 | bytes 1049600 | tf_op jit(solution)/shard_map/reduce_sum | solution.py:85
  80.0 1.6 %fusion.39 = f32[3,256]{1,0:T(4,128)S(1)} fusion(bf16[3,2048]{1,0:T(4,128)(2,1)S(1)} %get-tuple-element.6, bf16[256,2048]{1,0:T(8,128)(2,1)} %all-gather.3.cloned.1.call-done), kind=kOutput, calls=%fused_computation.44 | convolution fusion | flops 3145728 | bytes 1063936 | tf_op jit(solution)/shard_map/dot_general | solution.py:16
  81.6 9.1 %all-reduce = (f32[3,256]{1,0:T(4,128)S(1)}, f32[256]{0:T(256)S(1)}, f32[3]{0:T(128)S(1)}) all-reduce(f32[3,256]{1,0:T(4,128)S(1)} %fusion.39, f32[256]{0:T(256)S(1)} %multiply_reduce_fusion, f32[3]{0:T(128)S(1)} %get-tuple-element.5), channel_id=1, replica_groups=mesh['feat'=4,'dp'=8] {'feat'}, use_global_device_ids=true, to_apply=%region_1.2 | all-reduce | flops 1027 | bytes 8216 | tf_op jit(solution)/shard_map/psum | solution.py:88
  90.7 0.8 fusion.20
  91.5 0.0 copy-done.1
  (10 shorter events, 0.1 us)
Async XLA Ops:
  8.0 9.9 %copy-start = (bf16[1,128,128]{2,1,0:T(8,128)(2,1)S(1)}, bf16[1,128,128]{2,1,0:T(8,128)(2,1)}, u32[]{:S(2)}) copy-start(bf16[1,128,128]{2,1,0:T(8,128)(2,1)} %param.18) | copy-start | bytes 98308
  8.0 68.7 %reduce-scatter.4.cloned.1.call-start = ((), (), s32[]{:S(2)}) async-start(), calls=%async_computation.2 | async-start | bytes 5242880
  9.7 4.4 %copy-start.4 = (bf16[1,128,5120]{2,1,0:T(8,128)(2,1)S(1)}, bf16[1,128,5120]{2,1,0:T(8,128)(2,1)}, u32[]{:S(2)}) copy-start(bf16[1,128,5120]{2,1,0:T(8,128)(2,1)} %param.13) | copy-start | bytes 3932164
  9.7 4.4 %copy-start.5 = (bf16[1,5120,64]{1,2,0:T(8,128)(2,1)S(1)}, bf16[1,5120,64]{1,2,0:T(8,128)(2,1)}, u32[]{:S(2)}) copy-start(bf16[1,5120,64]{1,2,0:T(8,128)(2,1)} %param.16) | copy-start | bytes 1966084
  14.2 3.6 %copy-start.6 = (s32[3]{0:T(128)S(1)}, s32[3]{0:T(128)}, u32[]{:S(2)}) copy-start(s32[3]{0:T(128)} %param.19) | copy-start | bytes 40
  14.2 3.9 %copy-start.2 = (bf16[1,128,128]{2,1,0:T(8,128)(2,1)S(1)}, bf16[1,128,128]{2,1,0:T(8,128)(2,1)}, u32[]{:S(2)}) copy-start(bf16[1,128,128]{2,1,0:T(8,128)(2,1)} %param.17) | copy-start | bytes 98308
  21.2 0.7 copy-start.3
  21.3 57.3 %all-gather.3.cloned.1.call-start = ((), (), s32[]{:S(2)}) async-start(), calls=%async_computation.1 | async-start | bytes 1179648 | tf_op jit(solution)/shard_map/all_gather | solution.py:81
  78.5 13.0 %copy-start.1 = (bf16[3,2048]{1,0:T(4,128)(2,1)}, bf16[3,2048]{1,0:T(4,128)(2,1)S(1)}, u32[]{:S(2)}) copy-start(bf16[3,2048]{1,0:T(4,128)(2,1)S(1)} %get-tuple-element.6) | copy-start | bytes 36868
Sparse Core Ops, SparseCore 0:
  21.4 55.3 reduce-scatter.3
Sparse Core Ops, SparseCore 1:
  23.3 24.8 all-gather.2
where the time goes:
time: 99.3 us; the launch traced here: 99 us
  waiting for transfers between devices  40.7 us (41%)
  blocking collectives  23.5 us (24%)
  between operations  15.7 us (16%)
  matrix products  10.9 us (11%)
  local copies, waits for them, and re-layouts  6.05 us (6%)
  other arithmetic  2.02 us (2%)
    unnamed x3, waiting for transfers between devices  40.7 us
    all_gather x1, blocking collectives, local(): shard_marks = lax.all_gather(local_marks, 'dp', axis=0, tiled=True)  14.5 us
    psum x1, blocking collectives, local(): lax.psum((inner_block, train_part, norm_block), 'feat')  9.06 us
    dot_general x1, matrix products, local(): jnp.dot(grads_two, grad_weights, preferred_element_type=jnp.float32)  4.35 us
    unnamed x17, local copies, waits for them, and re-layouts  4.34 us
    dot_general x1, matrix products, local(): jnp.dot(inputs_two, input_weights, preferred_element_type=jnp.float32)  3.58 us
  transfers between devices with their start and end apart: 2, of which 1 were waited for; matrix products, arithmetic and copies ran while one was open for 2% of the time, Pallas kernels for 0%

commit v1 on v0

v1 whole, which is shorter than its diff:
```python
import functools
import math

import jax
import jax.numpy as jnp
from jax import lax
from jax.experimental import pallas as pl
from jax.experimental.pallas import tpu as pltpu
from jax.sharding import PartitionSpec as P

PROJ = 8192
DOMAINS = 8
LANES = 128

norm_eps = 1e-06

NT = (((1,), (1,)), ((), ()))
NN = (((1,), (0,)), ((), ()))
TN = (((0,), (0,)), ((), ()))


def dot32(left, right, dims, precision=None):
    return lax.dot_general(
        left, right, dims, precision=precision, preferred_element_type=jnp.float32
    )


def project_kernel(
    feat_size,
    steps,
    index_ref,
    counts_ref,
    x_ref,
    g_ref,
    a_ref,
    b_ref,
    of_ref,
    if_ref,
    rb_ref,
    ra_ref,
    *rest,
):
    outs = rest[:feat_size]
    acc_x, acc_b, acc_o, terms = rest[feat_size:]
    step = pl.program_id(0)
    rank = a_ref.shape[0]
    rows = of_ref.shape[0]
    examples = terms.shape[0]
    seq = acc_x.shape[0] // examples

    @pl.when(step == 0)
    def _():
        acc_x[...] = jnp.zeros_like(acc_x)
        acc_b[...] = jnp.zeros_like(acc_b)
        acc_o[...] = jnp.zeros_like(acc_o)

    weights_x = jnp.concatenate([a_ref[...], if_ref[...]], axis=0)
    acc_x[...] += dot32(x_ref[...], weights_x, NT)
    acc_b[...] += dot32(g_ref[...], b_ref[...], NN)
    acc_o[...] += dot32(g_ref[...], of_ref[...], NT)

    @pl.when(step == steps - 1)
    def _():
        hidden = acc_x[:, :rank].astype(jnp.bfloat16)
        back = acc_b[...].astype(jnp.bfloat16)
        hidden_rank = dot32(hidden, rb_ref[...], NN).astype(jnp.bfloat16)
        back_rank = dot32(back, ra_ref[...], NN).astype(jnp.bfloat16)
        place = lax.broadcasted_iota(jnp.int32, (seq, rows), 0)
        for e in range(examples):
            span = slice(e * seq, (e + 1) * seq)
            live = place < counts_ref[e]
            gp = jnp.where(live, acc_o[span, :], 0.0).astype(jnp.bfloat16)
            ip = jnp.where(live, acc_x[span, rank:], 0.0).astype(jnp.bfloat16)
            terms[e] = dot32(gp, hidden_rank[span], TN) + dot32(ip, back_rank[span], TN)
        part = rows // feat_size
        here = index_ref[0]
        for s in range(feat_size):
            owner = lax.rem(here + s, feat_size)
            start = pl.multiple_of(owner * part, part)
            outs[s][...] = terms[:, pl.ds(start, part), :]


def project(index, counts, x, g, a, b, of_t, if_t, rb, ra, feat_size, examples):
    tokens, width = x.shape
    rank = a.shape[0]
    rows = of_t.shape[0]
    cols = rb.shape[1]
    steps = 10
    kb = width // steps
    part = rows // feat_size
    smem = pl.BlockSpec(memory_space=pltpu.SMEM)
    whole = lambda shape: pl.BlockSpec(shape, lambda k: (0,) * len(shape))
    return pl.pallas_call(
        functools.partial(project_kernel, feat_size, steps),
        grid=(steps,),
        in_specs=[
            smem,
            smem,
            pl.BlockSpec((tokens, kb), lambda k: (0, k)),
            pl.BlockSpec((tokens, kb), lambda k: (0, k)),
            pl.BlockSpec((rank, kb), lambda k: (0, k)),
            pl.BlockSpec((kb, rank), lambda k: (k, 0)),
            pl.BlockSpec((rows, kb), lambda k: (0, k)),
            pl.BlockSpec((rows, kb), lambda k: (0, k)),
            whole(rb.shape),
            whole(ra.shape),
        ],
        out_specs=[whole((examples, part, cols))] * feat_size,
        out_shape=[jax.ShapeDtypeStruct((examples, part, cols), jnp.float32)] * feat_size,
        scratch_shapes=[
            pltpu.VMEM((tokens, rank + rows), jnp.float32),
            pltpu.VMEM((tokens, rank), jnp.float32),
            pltpu.VMEM((tokens, rows), jnp.float32),
            pltpu.VMEM((examples, rows, cols), jnp.float32),
        ],
        cost_estimate=pl.CostEstimate(
            flops=4 * tokens * width * (rank + rows),
            bytes_accessed=2 * (2 * tokens + 2 * rank + 2 * rows) * width,
            transcendentals=0,
        ),
        compiler_params=pltpu.CompilerParams(dimension_semantics=("arbitrary",)),
        name="project",
    )(index, counts, x, g, a, b, of_t, if_t, rb, ra)


def norms_kernel(near_ref, far_ref, out_ref):
    width = near_ref.shape[1] - LANES
    half = near_ref.shape[0]
    ones = jnp.ones((8, LANES), jnp.float32)
    for which, ref in enumerate((near_ref, far_ref)):
        total = jnp.zeros((half, LANES), jnp.float32)
        for c in range(0, width, LANES):
            piece = ref[:, c : c + LANES].astype(jnp.float32)
            total = total + piece * piece
        out_ref[:, which * half : (which + 1) * half] = dot32(
            ones, total, NT, lax.Precision.HIGHEST
        )


def combine_kernel(feat_size, counts_ref, *rest):
    blocks = rest[:feat_size]
    near_ref, far_ref, norms_ref, feat_ref, pack_ref, flat = rest[feat_size:]
    summed = blocks[0][...]
    for ref in blocks[1:]:
        summed = summed + ref[...]
    examples, part, cols = summed.shape
    half = near_ref.shape[0]
    pack_ref[...] = jnp.zeros_like(pack_ref)
    flat[...] = jnp.zeros_like(flat)
    for e in range(examples):
        value = (summed[e] / counts_ref[e].astype(jnp.float32)).astype(jnp.bfloat16)
        value = value.astype(jnp.float32)
        for k in range(part):
            flat[e : e + 1, k * cols : (k + 1) * cols] = value[k : k + 1, :]
    flat_value = flat[...]
    features = flat_value.astype(jnp.bfloat16)
    feat_ref[...] = features[:examples]
    norm = jnp.sum(flat_value * flat_value, axis=1, keepdims=True)
    width = part * cols
    inner_near = dot32(features, near_ref[:, :width], NT)
    inner_far = dot32(features, far_ref[:, :width], NT)
    pack_ref[:8, :half] = inner_near
    pack_ref[:8, half:] = inner_far
    pack_ref[8:16, :] = norms_ref[...]
    pack_ref[16:24, :] = jnp.broadcast_to(norm, pack_ref[16:24, :].shape)


def score_kernel(feat_size, scale, *rest):
    packs = rest[:feat_size]
    near_ref, far_ref, out_ref = rest[feat_size:]
    total = packs[0][...]
    for ref in packs[1:]:
        total = total + ref[...]
    half = near_ref.shape[0]
    examples = out_ref.shape[0]
    cosine = (
        total[:8]
        * lax.rsqrt(total[16:24] + norm_eps)
        * lax.rsqrt(total[8:16] + norm_eps)
    )
    ones = jnp.ones((8, half), jnp.float32)
    sums = jnp.zeros((8, LANES), jnp.float32)
    sizes = jnp.zeros((8, LANES), jnp.float32)
    for which, ref in enumerate((near_ref, far_ref)):
        ids = ref[...].astype(jnp.float32)
        lane = lax.broadcasted_iota(jnp.int32, ids.shape, 1).astype(jnp.float32)
        marks = jnp.where(ids == lane, 1.0, 0.0)
        piece = cosine[:, which * half : (which + 1) * half]
        sums = sums + dot32(piece, marks, NN, lax.Precision.HIGHEST)
        sizes = sizes + dot32(ones, marks, NN)
    out_ref[...] = (scale * sums / sizes)[:examples, : out_ref.shape[1]]


def shifted(value, axis, size, shift, stride=1):
    pairs = []
    for i in range(size):
        chip, core = divmod(i, stride)
        chips = size // stride
        pairs.append((i, ((chip + shift) % chips) * stride + core))
    return lax.ppermute(value, axis, pairs)


def local(
    feat_size,
    dp_size,
    layer_inputs,
    output_grads,
    adapter_a,
    adapter_b,
    out_factor,
    in_factor,
    rank_factor_b,
    rank_factor_a,
    token_counts,
    val_grads,
    val_domain,
):
    _, examples, seq_len, width = layer_inputs.shape
    val_rows, val_cols = val_grads.shape
    ids = jnp.broadcast_to(val_domain.astype(jnp.bfloat16), (val_rows, LANES))
    payload = jnp.concatenate([val_grads, ids], axis=1)
    chips = dp_size // 2
    pieces = [payload]
    for s in range(1, chips):
        pieces.append(shifted(payload, "dp", dp_size, s, 2))
    near = jnp.concatenate(pieces, axis=0)
    far = lax.ppermute(near, "dp", [(i, i ^ 1) for i in range(dp_size)])

    index = lax.axis_index("feat").astype(jnp.int32).reshape(1)
    blocks = project(
        index,
        token_counts,
        layer_inputs.reshape(examples * seq_len, width),
        output_grads.reshape(examples * seq_len, width),
        adapter_a[0],
        adapter_b[0],
        out_factor[0].T,
        in_factor[0].T,
        rank_factor_b[0],
        rank_factor_a[0],
        feat_size,
        examples,
    )
    held = [blocks[0]]
    for s in range(1, feat_size):
        held.append(shifted(blocks[s], "feat", feat_size, s))

    total_rows = 2 * near.shape[0]
    norms = pl.pallas_call(
        norms_kernel,
        out_shape=jax.ShapeDtypeStruct((8, total_rows), jnp.float32),
        name="norms",
    )(near, far)
    smem = pl.BlockSpec(memory_space=pltpu.SMEM)
    vmem = pl.BlockSpec(memory_space=pltpu.VMEM)
    train_features, pack = pl.pallas_call(
        functools.partial(combine_kernel, feat_size),
        in_specs=[smem] + [vmem] * (feat_size + 3),
        out_shape=[
            jax.ShapeDtypeStruct((examples, val_cols), jnp.bfloat16),
            jax.ShapeDtypeStruct((24, total_rows), jnp.float32),
        ],
        scratch_shapes=[pltpu.VMEM((8, val_cols), jnp.float32)],
        name="combine",
    )(token_counts, *held, near, far, norms)

    packs = [pack]
    for s in range(1, feat_size):
        packs.append(shifted(pack, "feat", feat_size, s))
    tail = pl.BlockSpec((near.shape[0], LANES), lambda i: (0, val_cols // LANES))
    whole = pl.BlockSpec(pack.shape, lambda i: (0, 0))
    domain_scores = pl.pallas_call(
        functools.partial(score_kernel, feat_size, math.sqrt(PROJ)),
        grid=(1,),
        in_specs=[whole] * feat_size + [tail, tail],
        out_specs=pl.BlockSpec((examples, DOMAINS), lambda i: (0, 0)),
        out_shape=jax.ShapeDtypeStruct((examples, DOMAINS), jnp.float32),
        name="score",
    )(*packs, near, far)
    return (train_features, domain_scores)


def solution(mesh):
    in_specs = (
        P("feat", "dp", None, None),
        P("feat", "dp", None, None),
        P("feat", None, None),
        P("feat", None, None),
        P("feat", None, None),
        P("feat", None, None),
        P("feat", None, None),
        P("feat", None, None),
        P("dp"),
        P("dp", "feat"),
        P("dp", None),
    )
    out_specs = (P("dp", "feat"), P("dp", None))
    body = functools.partial(local, mesh.shape["feat"], mesh.shape["dp"])
    return jax.shard_map(body, mesh=mesh, in_specs=in_specs, out_specs=out_specs, check_vma=False)
```

time: 99.3 us -> 51.4 us (0.52)
  waiting for transfers between devices: 40.7 us -> 15.5 us
  blocking collectives: 23.5 us -> 0 us
  Pallas kernels: 0 us -> 16.9 us
  between operations: 15.7 us -> 0.7 us
  starting transfers between devices: 0.08 us -> 13.2 us
  matrix products: 10.9 us -> 0 us
  local copies, waits for them, and re-layouts: 6.05 us -> 2.08 us
    unnamed x3 -> x0, waiting for transfers between devices: 40.7 us -> none
    pallas_call x0 -> x4, Pallas kernels: none -> 16.9 us  [the longest x1 10.6 us: project(): pl.pallas_call(functools.partial(project_kernel, feat_size, steps), grid=...]
    ppermute x0 -> x10, waiting for transfers between devices: none -> 15.5 us  [the longest x9 15.5 us: shifted(): return lax.ppermute(value, axis, pairs)]
    all_gather x1 -> x0, blocking collectives: 14.5 us -> none  [local(): shard_marks = lax.all_gather(local_marks, 'dp', axis=0, tiled=True)]
    ppermute x0 -> x10, starting transfers between devices: none -> 13.2 us  [the longest x9 13.2 us: shifted(): return lax.ppermute(value, axis, pairs)]
    dot_general x7 -> x0, matrix products: 10.9 us -> none  [the longest x1 4.35 us: local(): jnp.dot(grads_two, grad_weights, preferred_element_type=jnp.float32)]
    psum x1 -> x0, blocking collectives: 9.06 us -> none  [local(): lax.psum((inner_block, train_part, norm_block), 'feat')]
    unnamed x17 -> x16, local copies, waits for them, and re-layouts: 4.34 us -> 2.01 us
  transfers between devices with their start and end apart: 2 -> 10, of which waited for: 1 -> 5; matrix products, arithmetic and copies ran while one was open for 2% -> 0% of each run, Pallas kernels for 0% -> 25%
where the time goes in v1:
time: 51.4 us; the launch traced here: 50.9 us
  Pallas kernels  16.9 us (33%)
  waiting for transfers between devices  15.5 us (30%)
  starting transfers between devices  13.2 us (26%)
  other arithmetic  2.52 us (5%)
  local copies, waits for them, and re-layouts  2.08 us (4%)
  between operations  0.7 us (1%)
    ppermute x9, waiting for transfers between devices, shifted(): return lax.ppermute(value, axis, pairs)  15.5 us
    ppermute x9, starting transfers between devices, shifted(): return lax.ppermute(value, axis, pairs)  13.2 us
    pallas_call x1, Pallas kernels, project(): pl.pallas_call(functools.partial(project_kernel, feat_size, steps), grid=...  10.6 us
    pallas_call x1, Pallas kernels, local(): pl.pallas_call(norms_kernel, out_shape=jax.ShapeDtypeStruct((8, total_row...  2.32 us
    pallas_call x1, Pallas kernels, local(): pl.pallas_call(functools.partial(combine_kernel, feat_size), in_specs=[sm...  2.29 us
    unnamed x16, local copies, waits for them, and re-layouts  2.01 us
    pallas_call x1, Pallas kernels, local(): pl.pallas_call(functools.partial(score_kernel, feat_size, math.sqrt(PROJ)...  1.66 us
  transfers between devices with their start and end apart: 10, of which 5 were waited for; matrix products, arithmetic and copies ran while one was open for 0% of the time, Pallas kernels for 25%

profile of v1, /device:TPU:0, one launch (start us, length us, event | category | flops | bytes accessed | tf_op | source)
XLA Modules:
  0.0 50.9 jit_solution(11995056603919475590)
XLA Ops:
  0.6 0.7 %convert_bitcast_fusion = bf16[32]{0:T(256)(128)(2,1)S(1)} fusion(s32[32,1]{0,1:T(1,128)} %param.21), kind=kLoop, calls=%fused_computation.2 | loop fusion | flops 32 | bytes 192 | tf_op jit(solution)/shard_map/broadcast_in_dim | solution.py:220
  1.3 0.1 broadcast_in_dim.8
  1.4 0.9 %pad_maximum_fusion.1 = bf16[32,2176]{1,0:T(8,128)(2,1)S(1)} fusion(bf16[32,128]{1,0:T(8,128)(2,1)S(1)} %broadcast_in_dim.8, bf16[32,2048]{1,0:T(8,128)(2,1)} %param.20), kind=kLoop, calls=%fused_computation.1 | loop fusion | flops 278528 | bytes 278528 | tf_op jit(solution)/shard_map/concatenate | solution.py:221
  2.3 5.1 %collective-permute-start.5 = (bf16[32,2176]{1,0:T(8,128)(2,1)S(1)}, bf16[32,2176]{1,0:T(8,128)(2,1)S(1)}, u32[]{:S(2)}, u32[]{:S(2)}) collective-permute-start(bf16[32,2176]{1,0:T(8,128)(2,1)S(1)} %pad_maximum_fusion.1), channel_id=1, source_target_pairs={{0,6},{1,7},{2,0},{3,1},{4,2},{5,3},{6,4},{7,5},{8,14},{9,15},{10,... | collective-permute-start | bytes 417800 | tf_op jit(solution)/shard_map/ppermute | solution.py:200
  7.4 0.0 collective-permute-start.4
  7.4 1.0 %collective-permute-start.3 = (bf16[32,2176]{1,0:T(8,128)(2,1)S(1)}, bf16[32,2176]{1,0:T(8,128)(2,1)S(1)}, u32[]{:S(2)}, u32[]{:S(2)}) collective-permute-start(bf16[32,2176]{1,0:T(8,128)(2,1)S(1)} %pad_maximum_fusion.1), channel_id=1, source_target_pairs={{0,2},{1,3},{2,4},{3,5},{4,6},{5,7},{6,0},{7,1},{8,10},{9,11},{10,... | collective-permute-start | bytes 417800 | tf_op jit(solution)/shard_map/ppermute | solution.py:200
  8.4 3.1 %collective-permute-done.5 = bf16[32,2176]{1,0:T(8,128)(2,1)S(1)} collective-permute-done((bf16[32,2176]{1,0:T(8,128)(2,1)S(1)}, bf16[32,2176]{1,0:T(8,128)(2,1)S(1)}, u32[]{:S(2)}, u32[]{:S(2)}) %collective-permute-start.5) | collective-permute-done | bytes 139296 | tf_op jit(solution)/shard_map/ppermute | solution.py:200
  11.5 7.7 %collective-permute-done.4 = bf16[32,2176]{1,0:T(8,128)(2,1)S(1)} collective-permute-done((bf16[32,2176]{1,0:T(8,128)(2,1)S(1)}, bf16[32,2176]{1,0:T(8,128)(2,1)S(1)}, u32[]{:S(2)}, u32[]{:S(2)}) %collective-permute-start.4) | collective-permute-done | bytes 139296 | tf_op jit(solution)/shard_map/ppermute | solution.py:200
  19.2 0.0 collective-permute-done.3
  19.2 0.9 %pad_maximum_fusion.near_ref.rest_4_ = bf16[128,2176]{1,0:T(8,128)(2,1)S(1)} fusion(bf16[32,2176]{1,0:T(8,128)(2,1)S(1)} %collective-permute-done.5, bf16[32,2176]{1,0:T(8,128)(2,1)S(1)} %collective-permute-done.4, bf16[32,2176]{1,0:T(8,128)(2,1)S(1)} %collective-permute-done.3, bf16[32,128]{1,0:T(8,128)(2,1)S(1)} %broadcast_in_dim.8, bf16[32,2048]{1,0:T(8,128)(2,1)} %param.20), kind=kLoop, calls=%fused_computation | loop fusion | flops 2785280 | bytes 1114112 | tf_op jit(solution)/shard_map/concatenate | solution.py:226
  20.2 0.0 copy-start
  20.2 0.1 collective-permute-start.6
  20.3 10.6 %project.1 = (f32[3,16,128]{2,1,0:T(8,128)}, f32[3,16,128]{2,1,0:T(8,128)}, f32[3,16,128]{2,1,0:T(8,128)}, f32[3,16,128]{2,1,0:T(8,128)}) custom-call(s32[1]{0:T(128)} %bitcast.index_ref, s32[3]{0:T(128)} %counts_ref.3, bf16[384,5120]{1,0:T(8,128)(2,1)} %bitcast.15, bf16[384,5120]{1,0:T(8,128)(2,1)} %bitcast.16, bf16[128,5120]{1,0:T(8,128)(2,1)} %bitcast.17, ...), custom_call_target="tpu_custom_call" | custom-call | flops 1509949440 | bytes 11796480 | tf_op jit(solution)/shard_map/project/pallas_call | solution.py:93
  30.9 0.0 copy-done
  30.9 1.5 %collective-permute-start = (f32[3,16,128]{2,1,0:T(8,128)}, f32[3,16,128]{2,1,0:T(8,128)S(1)}, u32[]{:S(2)}, u32[]{:S(2)}) collective-permute-start(f32[3,16,128]{2,1,0:T(8,128)} %get-tuple-element.9), channel_id=1, source_target_pairs={{0,8},{8,16},{16,24},{24,0},{1,9},{9,17},{17,25},{25,1},{2,10},{10... | collective-permute-start | bytes 73736 | tf_op jit(solution)/shard_map/ppermute | solution.py:200
  32.4 1.5 %collective-permute-start.1 = (f32[3,16,128]{2,1,0:T(8,128)}, f32[3,16,128]{2,1,0:T(8,128)S(1)}, u32[]{:S(2)}, u32[]{:S(2)}) collective-permute-start(f32[3,16,128]{2,1,0:T(8,128)} %get-tuple-element.10), channel_id=1, source_target_pairs={{0,16},{8,24},{16,0},{24,8},{1,17},{9,25},{17,1},{25,9},{2,18},{10... | collective-permute-start | bytes 73736 | tf_op jit(solution)/shard_map/ppermute | solution.py:200
  34.0 1.4 %collective-permute-start.2 = (f32[3,16,128]{2,1,0:T(8,128)}, f32[3,16,128]{2,1,0:T(8,128)S(1)}, u32[]{:S(2)}, u32[]{:S(2)}) collective-permute-start(f32[3,16,128]{2,1,0:T(8,128)} %get-tuple-element.11), channel_id=1, source_target_pairs={{0,24},{8,0},{16,8},{24,16},{1,25},{9,1},{17,9},{25,17},{2,26},{10... | collective-permute-start | bytes 73736 | tf_op jit(solution)/shard_map/ppermute | solution.py:200
  35.4 0.0 collective-permute-done.6.far_ref.rest_5_
  35.4 0.0 copy-start.1
  35.4 0.8 %copy-done.1 = bf16[128,2176]{1,0:T(8,128)(2,1)} copy-done((bf16[128,2176]{1,0:T(8,128)(2,1)}, bf16[128,2176]{1,0:T(8,128)(2,1)S(1)}, u32[]{:S(2)}) %copy-start.1) | copy-done | bytes 557080
  36.2 2.3 %norms.1.rest_6_ = f32[8,256]{1,0:T(8,128)} custom-call(bf16[128,2176]{1,0:T(8,128)(2,1)} %copy-done, bf16[128,2176]{1,0:T(8,128)(2,1)} %copy-done.1), custom_call_target="tpu_custom_call" | custom-call | tf_op jit(solution)/shard_map/norms/pallas_call | solution.py:249
  38.5 0.0 collective-permute-done.rest_1_
  38.5 0.0 copy-start.2
  38.5 0.0 collective-permute-done.1.rest_2_
  38.5 0.0 copy-start.3
  38.5 0.0 collective-permute-done.2.rest_3_
  38.6 0.0 copy-start.4
  38.6 0.6 %copy-done.2 = f32[3,16,128]{2,1,0:T(8,128)} copy-done((f32[3,16,128]{2,1,0:T(8,128)}, f32[3,16,128]{2,1,0:T(8,128)S(1)}, u32[]{:S(2)}) %copy-start.2) | copy-done | bytes 24600
  39.1 0.0 copy-done.3
  39.1 0.0 copy-done.4
  39.2 2.3 %combine.1 = (bf16[3,2048]{1,0:T(4,128)(2,1)}, f32[24,256]{1,0:T(8,128)}) custom-call(s32[3]{0:T(128)} %counts_ref.3, f32[3,16,128]{2,1,0:T(8,128)} %get-tuple-element.8.rest_0_, f32[3,16,128]{2,1,0:T(8,128)} %copy-done.2, f32[3,16,128]{2,1,0:T(8,128)} %copy-done.3, f32[3,16,128]{2,1,0:T(8,128)} %copy-done.4, bf16[128,2176]{1,0:T(8,128)(2,1)} %copy-done, ...), custom_call_target="tpu_custom_call" | custom-call | tf_op jit(solution)/shard_map/combine/pallas_call | solution.py:256
  41.4 1.8 %collective-permute-start.9 = (f32[24,256]{1,0:T(8,128)}, f32[24,256]{1,0:T(8,128)S(1)}, u32[]{:S(2)}, u32[]{:S(2)}) collective-permute-start(f32[24,256]{1,0:T(8,128)} %get-tuple-element.13.rest_0_), channel_id=1, source_target_pairs={{0,24},{8,0},{16,8},{24,16},{1,25},{9,1},{17,9},{25,17},{2,26},{10... | collective-permute-start | bytes 73736 | tf_op jit(solution)/shard_map/ppermute | solution.py:200
  43.2 0.5 collective-permute-start.8
  43.7 0.2 collective-permute-start.7
  44.0 1.5 %collective-permute-done.9.rest_3_ = f32[24,256]{1,0:T(8,128)S(1)} collective-permute-done((f32[24,256]{1,0:T(8,128)}, f32[24,256]{1,0:T(8,128)S(1)}, u32[]{:S(2)}, u32[]{:S(2)}) %collective-permute-start.9) | collective-permute-done | bytes 24608 | tf_op jit(solution)/shard_map/ppermute | solution.py:200
  45.5 0.0 copy-start.5
  45.5 1.8 %collective-permute-done.8.rest_2_ = f32[24,256]{1,0:T(8,128)S(1)} collective-permute-done((f32[24,256]{1,0:T(8,128)}, f32[24,256]{1,0:T(8,128)S(1)}, u32[]{:S(2)}, u32[]{:S(2)}) %collective-permute-start.8) | collective-permute-done | bytes 24608 | tf_op jit(solution)/shard_map/ppermute | solution.py:200
  47.3 0.0 copy-start.6
  47.3 1.4 %collective-permute-done.7.rest_1_ = f32[24,256]{1,0:T(8,128)S(1)} collective-permute-done((f32[24,256]{1,0:T(8,128)}, f32[24,256]{1,0:T(8,128)S(1)}, u32[]{:S(2)}, u32[]{:S(2)}) %collective-permute-start.7) | collective-permute-done | bytes 24608 | tf_op jit(solution)/shard_map/ppermute | solution.py:200
  48.7 0.0 copy-done.5
  48.7 0.0 copy-done.6
  48.7 0.0 copy-start.7
  48.7 0.6 %copy-done.7 = f32[24,256]{1,0:T(8,128)} copy-done((f32[24,256]{1,0:T(8,128)}, f32[24,256]{1,0:T(8,128)S(1)}, u32[]{:S(2)}) %copy-start.7) | copy-done | bytes 24600
  49.3 1.7 %score.1 = f32[3,8]{1,0:T(4,128)} custom-call(f32[24,256]{1,0:T(8,128)} %get-tuple-element.13.rest_0_, f32[24,256]{1,0:T(8,128)} %copy-done.7, f32[24,256]{1,0:T(8,128)} %copy-done.6, f32[24,256]{1,0:T(8,128)} %copy-done.5, bf16[128,2176]{1,0:T(8,128)(2,1)} %copy-done, bf16[128,2176]{1,0:T(8,128)(2,1)} %copy-done.1), custom_call_target="tpu_custom_call" | custom-call | tf_op jit(solution)/shard_map/score/pallas_call | solution.py:272
Async XLA Ops:
  2.3 9.2 %collective-permute-start.5 = (bf16[32,2176]{1,0:T(8,128)(2,1)S(1)}, bf16[32,2176]{1,0:T(8,128)(2,1)S(1)}, u32[]{:S(2)}, u32[]{:S(2)}) collective-permute-start(bf16[32,2176]{1,0:T(8,128)(2,1)S(1)} %pad_maximum_fusion.1), channel_id=1, source_target_pairs={{0,6},{1,7},{2,0},{3,1},{4,2},{5,3},{6,4},{7,5},{8,14},{9,15},{10,... | collective-permute-start | bytes 417800 | tf_op jit(solution)/shard_map/ppermute | solution.py:200
  7.4 11.8 %collective-permute-start.4 = (bf16[32,2176]{1,0:T(8,128)(2,1)S(1)}, bf16[32,2176]{1,0:T(8,128)(2,1)S(1)}, u32[]{:S(2)}, u32[]{:S(2)}) collective-permute-start(bf16[32,2176]{1,0:T(8,128)(2,1)S(1)} %pad_maximum_fusion.1), channel_id=1, source_target_pairs={{0,4},{1,5},{2,6},{3,7},{4,0},{5,1},{6,2},{7,3},{8,12},{9,13},{10,... | collective-permute-start | bytes 417800 | tf_op jit(solution)/shard_map/ppermute | solution.py:200
  7.4 11.8 %collective-permute-start.3 = (bf16[32,2176]{1,0:T(8,128)(2,1)S(1)}, bf16[32,2176]{1,0:T(8,128)(2,1)S(1)}, u32[]{:S(2)}, u32[]{:S(2)}) collective-permute-start(bf16[32,2176]{1,0:T(8,128)(2,1)S(1)} %pad_maximum_fusion.1), channel_id=1, source_target_pairs={{0,2},{1,3},{2,4},{3,5},{4,6},{5,7},{6,0},{7,1},{8,10},{9,11},{10,... | collective-permute-start | bytes 417800 | tf_op jit(solution)/shard_map/ppermute | solution.py:200
  20.2 10.7 %copy-start = (bf16[128,2176]{1,0:T(8,128)(2,1)}, bf16[128,2176]{1,0:T(8,128)(2,1)S(1)}, u32[]{:S(2)}) copy-start(bf16[128,2176]{1,0:T(8,128)(2,1)S(1)} %pad_maximum_fusion.near_ref.rest_4_) | copy-start | bytes 1671172
  20.2 15.2 %collective-permute-start.6 = (bf16[128,2176]{1,0:T(8,128)(2,1)S(1)}, bf16[128,2176]{1,0:T(8,128)(2,1)S(1)}, u32[]{:S(2)}, u32[]{:S(2)}) collective-permute-start(bf16[128,2176]{1,0:T(8,128)(2,1)S(1)} %pad_maximum_fusion.near_ref.rest_4_), channel_id=1, source_target_pairs={{0,1},{1,0},{2,3},{3,2},{4,5},{5,4},{6,7},{7,6},{8,9},{9,8},{10,11... | collective-permute-start | bytes 1671176 | tf_op jit(solution)/shard_map/ppermute | solution.py:227
  30.9 7.6 %collective-permute-start = (f32[3,16,128]{2,1,0:T(8,128)}, f32[3,16,128]{2,1,0:T(8,128)S(1)}, u32[]{:S(2)}, u32[]{:S(2)}) collective-permute-start(f32[3,16,128]{2,1,0:T(8,128)} %get-tuple-element.9), channel_id=1, source_target_pairs={{0,8},{8,16},{16,24},{24,0},{1,9},{9,17},{17,25},{25,1},{2,10},{10... | collective-permute-start | bytes 73736 | tf_op jit(solution)/shard_map/ppermute | solution.py:200
  32.4 6.1 %collective-permute-start.1 = (f32[3,16,128]{2,1,0:T(8,128)}, f32[3,16,128]{2,1,0:T(8,128)S(1)}, u32[]{:S(2)}, u32[]{:S(2)}) collective-permute-start(f32[3,16,128]{2,1,0:T(8,128)} %get-tuple-element.10), channel_id=1, source_target_pairs={{0,16},{8,24},{16,0},{24,8},{1,17},{9,25},{17,1},{25,9},{2,18},{10... | collective-permute-start | bytes 73736 | tf_op jit(solution)/shard_map/ppermute | solution.py:200
  34.0 4.6 %collective-permute-start.2 = (f32[3,16,128]{2,1,0:T(8,128)}, f32[3,16,128]{2,1,0:T(8,128)S(1)}, u32[]{:S(2)}, u32[]{:S(2)}) collective-permute-start(f32[3,16,128]{2,1,0:T(8,128)} %get-tuple-element.11), channel_id=1, source_target_pairs={{0,24},{8,0},{16,8},{24,16},{1,25},{9,1},{17,9},{25,17},{2,26},{10... | collective-permute-start | bytes 73736 | tf_op jit(solution)/shard_map/ppermute | solution.py:200
  35.4 0.8 %copy-start.1 = (bf16[128,2176]{1,0:T(8,128)(2,1)}, bf16[128,2176]{1,0:T(8,128)(2,1)S(1)}, u32[]{:S(2)}) copy-start(bf16[128,2176]{1,0:T(8,128)(2,1)S(1)} %collective-permute-done.6.far_ref.rest_5_) | copy-start | bytes 1671172
  38.5 0.6 %copy-start.2 = (f32[3,16,128]{2,1,0:T(8,128)}, f32[3,16,128]{2,1,0:T(8,128)S(1)}, u32[]{:S(2)}) copy-start(f32[3,16,128]{2,1,0:T(8,128)S(1)} %collective-permute-done.rest_1_) | copy-start | bytes 73732
  38.5 0.6 %copy-start.3 = (f32[3,16,128]{2,1,0:T(8,128)}, f32[3,16,128]{2,1,0:T(8,128)S(1)}, u32[]{:S(2)}) copy-start(f32[3,16,128]{2,1,0:T(8,128)S(1)} %collective-permute-done.1.rest_2_) | copy-start | bytes 73732
  38.6 0.6 %copy-start.4 = (f32[3,16,128]{2,1,0:T(8,128)}, f32[3,16,128]{2,1,0:T(8,128)S(1)}, u32[]{:S(2)}) copy-start(f32[3,16,128]{2,1,0:T(8,128)S(1)} %collective-permute-done.2.rest_3_) | copy-start | bytes 73732
  41.4 4.0 %collective-permute-start.9 = (f32[24,256]{1,0:T(8,128)}, f32[24,256]{1,0:T(8,128)S(1)}, u32[]{:S(2)}, u32[]{:S(2)}) collective-permute-start(f32[24,256]{1,0:T(8,128)} %get-tuple-element.13.rest_0_), channel_id=1, source_target_pairs={{0,24},{8,0},{16,8},{24,16},{1,25},{9,1},{17,9},{25,17},{2,26},{10... | collective-permute-start | bytes 73736 | tf_op jit(solution)/shard_map/ppermute | solution.py:200
  43.2 4.0 %collective-permute-start.8 = (f32[24,256]{1,0:T(8,128)}, f32[24,256]{1,0:T(8,128)S(1)}, u32[]{:S(2)}, u32[]{:S(2)}) collective-permute-start(f32[24,256]{1,0:T(8,128)} %get-tuple-element.13.rest_0_), channel_id=1, source_target_pairs={{0,16},{8,24},{16,0},{24,8},{1,17},{9,25},{17,1},{25,9},{2,18},{10... | collective-permute-start | bytes 73736 | tf_op jit(solution)/shard_map/ppermute | solution.py:200
  43.7 4.9 %collective-permute-start.7 = (f32[24,256]{1,0:T(8,128)}, f32[24,256]{1,0:T(8,128)S(1)}, u32[]{:S(2)}, u32[]{:S(2)}) collective-permute-start(f32[24,256]{1,0:T(8,128)} %get-tuple-element.13.rest_0_), channel_id=1, source_target_pairs={{0,8},{8,16},{16,24},{24,0},{1,9},{9,17},{17,25},{25,1},{2,10},{10... | collective-permute-start | bytes 73736 | tf_op jit(solution)/shard_map/ppermute | solution.py:200
  45.5 3.2 %copy-start.5 = (f32[24,256]{1,0:T(8,128)}, f32[24,256]{1,0:T(8,128)S(1)}, u32[]{:S(2)}) copy-start(f32[24,256]{1,0:T(8,128)S(1)} %collective-permute-done.9.rest_3_) | copy-start | bytes 73732
  47.3 1.4 %copy-start.6 = (f32[24,256]{1,0:T(8,128)}, f32[24,256]{1,0:T(8,128)S(1)}, u32[]{:S(2)}) copy-start(f32[24,256]{1,0:T(8,128)S(1)} %collective-permute-done.8.rest_2_) | copy-start | bytes 73732
  48.7 0.6 %copy-start.7 = (f32[24,256]{1,0:T(8,128)}, f32[24,256]{1,0:T(8,128)S(1)}, u32[]{:S(2)}) copy-start(f32[24,256]{1,0:T(8,128)S(1)} %collective-permute-done.7.rest_1_) | copy-start | bytes 73732

commit v2 on v1

v2 whole, which is shorter than its diff:
```python
import functools
import math

import jax
import jax.numpy as jnp
from jax import lax
from jax.experimental import pallas as pl
from jax.experimental.pallas import tpu as pltpu
from jax.sharding import Mesh
from jax.sharding import PartitionSpec as P

PROJ = 8192
DOMAINS = 8
LANES = 128
SUBLANES = 8

FAR = ("hi",)
NEAR = ("lo", "core")
DP = ("hi", "lo", "core")

norm_eps = 1e-06

NT = (((1,), (1,)), ((), ()))
NN = (((1,), (0,)), ((), ()))
TN = (((0,), (0,)), ((), ()))
HIGHEST = lax.Precision.HIGHEST


def dot32(left, right, dims, precision=None):
    return lax.dot_general(
        left, right, dims, precision=precision, preferred_element_type=jnp.float32
    )


def limit(mib):
    return pltpu.CompilerParams(vmem_limit_bytes=mib << 20)


def round_up(value, unit):
    return (value + unit - 1) // unit * unit


def payload_kernel(val_ref, domain_ref, out_ref):
    rows = val_ref.shape[0]
    out_ref[:rows, :] = val_ref[...]
    out_ref[rows:, :] = jnp.zeros_like(out_ref[rows:, :])
    ids = jnp.broadcast_to(domain_ref[...].astype(jnp.float32), (SUBLANES, rows))
    out_ref[rows : rows + SUBLANES, :rows] = ids.astype(jnp.bfloat16)


def project_kernel(
    steps,
    counts_ref,
    x_ref,
    g_ref,
    a_ref,
    b_ref,
    of_ref,
    if_ref,
    rb_ref,
    ra_ref,
    out_ref,
    acc_x,
    acc_b,
    acc_o,
):
    step = pl.program_id(0)
    rank = a_ref.shape[0]
    rows = of_ref.shape[0]
    feat_size, copies, examples, part, _ = out_ref.shape
    seq = acc_x.shape[0] // examples

    @pl.when(step == 0)
    def _():
        acc_x[...] = jnp.zeros_like(acc_x)
        acc_b[...] = jnp.zeros_like(acc_b)
        acc_o[...] = jnp.zeros_like(acc_o)

    weights_x = jnp.concatenate([a_ref[...], if_ref[...]], axis=0)
    acc_x[...] += dot32(x_ref[...], weights_x, NT)
    acc_b[...] += dot32(g_ref[...], b_ref[...], NN)
    acc_o[...] += dot32(g_ref[...], of_ref[...], NT)

    @pl.when(step == steps - 1)
    def _():
        hidden = acc_x[:, :rank].astype(jnp.bfloat16)
        back = acc_b[...].astype(jnp.bfloat16)
        hidden_rank = dot32(hidden, rb_ref[...], NN).astype(jnp.bfloat16)
        back_rank = dot32(back, ra_ref[...], NN).astype(jnp.bfloat16)
        place = lax.broadcasted_iota(jnp.int32, (seq, rows), 0)
        for e in range(examples):
            span = slice(e * seq, (e + 1) * seq)
            live = place < counts_ref[e]
            gp = jnp.where(live, acc_o[span, :], 0.0).astype(jnp.bfloat16)
            ip = jnp.where(live, acc_x[span, rank:], 0.0).astype(jnp.bfloat16)
            term = dot32(gp, hidden_rank[span], TN) + dot32(ip, back_rank[span], TN)
            term = (term / counts_ref[e].astype(jnp.float32)).astype(jnp.bfloat16)
            for f in range(feat_size):
                for q in range(copies):
                    out_ref[f, q, e] = term[f * part : (f + 1) * part]


def project(counts, x, g, a, b, of_t, if_t, rb, ra, feat_size, copies, examples):
    tokens, width = x.shape
    rank = a.shape[0]
    rows = of_t.shape[0]
    cols = rb.shape[1]
    steps = 10
    kb = width // steps
    part = rows // feat_size
    whole = lambda shape: pl.BlockSpec(shape, lambda k: (0,) * len(shape))
    out = (feat_size, copies, examples, part, cols)
    return pl.pallas_call(
        functools.partial(project_kernel, steps),
        grid=(steps,),
        in_specs=[
            pl.BlockSpec(memory_space=pltpu.SMEM),
            pl.BlockSpec((tokens, kb), lambda k: (0, k)),
            pl.BlockSpec((tokens, kb), lambda k: (0, k)),
            pl.BlockSpec((rank, kb), lambda k: (0, k)),
            pl.BlockSpec((kb, rank), lambda k: (k, 0)),
            pl.BlockSpec((rows, kb), lambda k: (0, k)),
            pl.BlockSpec((rows, kb), lambda k: (0, k)),
            whole(rb.shape),
            whole(ra.shape),
        ],
        out_specs=whole(out),
        out_shape=jax.ShapeDtypeStruct(out, jnp.bfloat16),
        scratch_shapes=[
            pltpu.VMEM((tokens, rank + rows), jnp.float32),
            pltpu.VMEM((tokens, rank), jnp.float32),
            pltpu.VMEM((tokens, rows), jnp.float32),
        ],
        cost_estimate=pl.CostEstimate(
            flops=4 * tokens * width * (rank + rows),
            bytes_accessed=2 * (2 * tokens + 2 * rank + 2 * rows) * width,
            transcendentals=0,
        ),
        compiler_params=limit(16),
        name="project",
    )(counts, x, g, a, b, of_t, if_t, rb, ra)


def combine_kernel(rows, index_ref, parts_ref, *rest):
    pieces = rest[:-4]
    feat_ref, pack_ref, summed, flat = rest[-4:]
    feat_size, copies, examples, part, cols = parts_ref.shape
    width = part * cols
    members = copies * examples
    total = parts_ref[0].astype(jnp.float32)
    for f in range(1, feat_size):
        total = total + parts_ref[f].astype(jnp.float32)
    summed[...] = total.reshape(members * part, cols)
    flat[...] = jnp.zeros_like(flat)
    mine = index_ref[0] * (examples * part)
    for k in range(part):
        span = slice(k * cols, (k + 1) * cols)
        flat[:members, span] = summed[pl.ds(k, members, stride=part), :]
        feat_ref[:, span] = summed[pl.ds(mine + k, examples, stride=part), :].astype(jnp.bfloat16)
    features = flat[...].astype(jnp.bfloat16)
    rounded = features.astype(jnp.float32)
    norm = jnp.sum(rounded * rounded, axis=1, keepdims=True)
    count = len(pieces) * rows
    vals = jnp.concatenate([ref[:rows, :] for ref in pieces], axis=0)
    inner = dot32(features, vals, NT)
    squares = jnp.zeros((count, LANES), jnp.float32)
    for c in range(0, width, LANES):
        piece = vals[:, c : c + LANES].astype(jnp.float32)
        squares = squares + piece * piece
    val_norm = dot32(jnp.ones((SUBLANES, LANES), jnp.float32), squares, NT, HIGHEST)
    ids = jnp.concatenate(
        [ref[rows : rows + SUBLANES, :rows].astype(jnp.float32) for ref in pieces], axis=1
    )
    pack_ref[...] = jnp.full(pack_ref.shape, -1.0, jnp.float32)
    lanes = pack_ref.shape[-1]
    for q in range(copies):
        span = slice(q * examples, (q + 1) * examples)
        wide = jnp.broadcast_to(norm[span], (examples, lanes))
        for f in range(feat_size):
            pack_ref[f, q, :examples, :count] = inner[span]
            pack_ref[f, q, examples : 2 * examples, :] = wide
            pack_ref[f, q, 2 * examples : 2 * examples + 1, :count] = val_norm[:1]
            pack_ref[f, q, 2 * examples + 1 : 2 * examples + 2, :count] = ids[:1]


def score_kernel(count, scale, packs_ref, out_ref):
    feat_size, copies, _, lanes = packs_ref.shape
    examples = out_ref.shape[0]
    total = packs_ref[0]
    for f in range(1, feat_size):
        total = total + packs_ref[f]
    inner = total[:, :examples, :count]
    norm = total[0, examples : 2 * examples, :count]
    val_norm = total[:, 2 * examples : 2 * examples + 1, :count]
    ids = packs_ref[0, :, 2 * examples + 1 : 2 * examples + 2, :count]
    root = lax.rsqrt(norm + norm_eps)
    sums = jnp.zeros((examples, DOMAINS), jnp.float32)
    sizes = jnp.zeros((examples, DOMAINS), jnp.float32)
    ones = jnp.ones((examples, count), jnp.float32)
    domain = lax.broadcasted_iota(jnp.int32, (DOMAINS, count), 0).astype(jnp.float32)
    for q in range(copies):
        cosine = inner[q] * root * lax.rsqrt(val_norm[q] + norm_eps)
        marks = jnp.where(jnp.broadcast_to(ids[q], domain.shape) == domain, 1.0, 0.0)
        sums = sums + dot32(cosine, marks, NT, HIGHEST)
        sizes = sizes + dot32(ones, marks, NT)
    out_ref[...] = scale * sums / sizes


def axis_count(sizes, names):
    total = 1
    for name in names:
        total *= sizes[name]
    return total


def local(
    sizes,
    layer_inputs,
    output_grads,
    adapter_a,
    adapter_b,
    out_factor,
    in_factor,
    rank_factor_b,
    rank_factor_a,
    token_counts,
    val_grads,
    val_domain,
):
    _, examples, seq_len, width = layer_inputs.shape
    val_rows, val_cols = val_grads.shape
    feat_size = sizes["feat"]
    copies = axis_count(sizes, NEAR)
    far_size = axis_count(sizes, FAR)

    payload = pl.pallas_call(
        payload_kernel,
        out_shape=jax.ShapeDtypeStruct((val_rows + SUBLANES, val_cols), jnp.bfloat16),
        compiler_params=limit(4),
        name="payload",
    )(val_grads, val_domain.T)
    pieces = [payload]
    for s in range(1, far_size):
        pairs = [(i, (i + s) % far_size) for i in range(far_size)]
        pieces.append(lax.ppermute(payload, FAR, pairs))

    parts = project(
        token_counts,
        layer_inputs.reshape(examples * seq_len, width),
        output_grads.reshape(examples * seq_len, width),
        adapter_a[0],
        adapter_b[0],
        out_factor[0].T,
        in_factor[0].T,
        rank_factor_b[0],
        rank_factor_a[0],
        feat_size,
        copies,
        examples,
    )
    group = ("feat",) + NEAR
    members = feat_size * copies
    flat_parts = parts.reshape((members,) + parts.shape[2:])
    got = lax.all_to_all(flat_parts, group, 0, 0, tiled=True).reshape(parts.shape)

    count = far_size * val_rows
    lanes = round_up(count, LANES)
    block_rows = round_up(2 * examples + 2, SUBLANES)
    part, cols = parts.shape[3:]
    index = lax.axis_index(NEAR).astype(jnp.int32).reshape(1)
    smem = pl.BlockSpec(memory_space=pltpu.SMEM)
    vmem = pl.BlockSpec(memory_space=pltpu.VMEM)
    train_features, packs = pl.pallas_call(
        functools.partial(combine_kernel, val_rows),
        in_specs=[smem] + [vmem] * (1 + far_size),
        out_shape=[
            jax.ShapeDtypeStruct((examples, val_cols), jnp.bfloat16),
            jax.ShapeDtypeStruct((feat_size, copies, block_rows, lanes), jnp.float32),
        ],
        scratch_shapes=[
            pltpu.VMEM((copies * examples * part, cols), jnp.float32),
            pltpu.VMEM((round_up(copies * examples, 2 * SUBLANES), val_cols), jnp.float32),
        ],
        compiler_params=limit(8),
        name="combine",
    )(index, got, *pieces)

    flat_packs = packs.reshape((members,) + packs.shape[2:])
    returned = lax.all_to_all(flat_packs, group, 0, 0, tiled=True).reshape(packs.shape)
    domain_scores = pl.pallas_call(
        functools.partial(score_kernel, count, math.sqrt(PROJ)),
        out_shape=jax.ShapeDtypeStruct((examples, DOMAINS), jnp.float32),
        compiler_params=limit(4),
        name="score",
    )(returned)
    return (train_features, domain_scores)


def solution(mesh):
    in_specs = (
        P("feat", DP, None, None),
        P("feat", DP, None, None),
        P("feat", None, None),
        P("feat", None, None),
        P("feat", None, None),
        P("feat", None, None),
        P("feat", None, None),
        P("feat", None, None),
        P(DP),
        P(DP, "feat"),
        P(DP, None),
    )
    out_specs = (P(DP, "feat"), P(DP, None))
    feat_size, dp_size = mesh.shape["feat"], mesh.shape["dp"]
    sizes = {"feat": feat_size, "hi": dp_size // 4, "lo": 2, "core": 2}
    split = Mesh(mesh.devices.reshape(tuple(sizes.values())), tuple(sizes))
    body = functools.partial(local, sizes)
    return jax.shard_map(body, mesh=split, in_specs=in_specs, out_specs=out_specs, check_vma=False)
```

time: 51.4 us -> 48.4 us (0.942)
  blocking collectives: 0 us -> 9.59 us
  local copies, waits for them, and re-layouts: 2.08 us -> 11.2 us
  Pallas kernels: 16.9 us -> 8.93 us
  waiting for transfers between devices: 15.5 us -> 8.38 us
  starting transfers between devices: 13.2 us -> 8.97 us
  other arithmetic: 2.52 us -> 0 us
    ppermute x10 -> x1, starting transfers between devices: 13.2 us -> 2.66 us  [local(): pieces.append(lax.ppermute(payload, FAR, pairs))]
    all_to_all x0 -> x1, blocking collectives: none -> 9.59 us  [local(): lax.all_to_all(flat_packs, group, 0, 0, tiled=True).reshape(packs.shape)]
    unnamed x16 -> x22, local copies, waits for them, and re-layouts: 2.01 us -> 11.2 us
    pallas_call x4, Pallas kernels: 16.9 us -> 8.93 us  [the longest x1 7.31 us: project(): pl.pallas_call(functools.partial(project_kernel, steps), grid=(steps,), i...]
    ppermute x10 -> x1, waiting for transfers between devices: 15.5 us -> 8.38 us  [local(): pieces.append(lax.ppermute(payload, FAR, pairs))]
    all_to_all x0 -> x1, starting transfers between devices: none -> 6.32 us  [local(): lax.all_to_all(flat_parts, group, 0, 0, tiled=True).reshape(parts.shape)]
    concatenate x2 -> x0, other arithmetic: 1.86 us -> none  [the longest x1 0.95 us: local(): near = jnp.concatenate(pieces, axis=0)]
    broadcast_in_dim x1 -> x0, other arithmetic: 0.66 us -> none  [local(): ids = jnp.broadcast_to(val_domain.astype(jnp.bfloat16), (val_rows, LANES))]
  transfers between devices with their start and end apart: 10 -> 2, of which waited for: 5 -> 1; matrix products, arithmetic and copies ran while one was open for 0% -> 0% of each run, Pallas kernels for 25% -> 0%
where the time goes in v2:
time: 48.4 us; the launch traced here: 47.8 us
  local copies, waits for them, and re-layouts  11.2 us (23%)
  blocking collectives  9.59 us (20%)
  starting transfers between devices  8.97 us (19%)
  Pallas kernels  8.93 us (18%)
  waiting for transfers between devices  8.38 us (17%)
  between operations  0.69 us (1%)
    unnamed x22, local copies, waits for them, and re-layouts  11.2 us
    all_to_all x1, blocking collectives, local(): lax.all_to_all(flat_packs, group, 0, 0, tiled=True).reshape(packs.shape)  9.59 us
    ppermute x1, waiting for transfers between devices, local(): pieces.append(lax.ppermute(payload, FAR, pairs))  8.38 us
    pallas_call x1, Pallas kernels, project(): pl.pallas_call(functools.partial(project_kernel, steps), grid=(steps,), i...  7.31 us
    all_to_all x1, starting transfers between devices, local(): lax.all_to_all(flat_parts, group, 0, 0, tiled=True).reshape(parts.shape)  6.32 us
    ppermute x1, starting transfers between devices, local(): pieces.append(lax.ppermute(payload, FAR, pairs))  2.66 us
  transfers between devices with their start and end apart: 2, of which 1 were waited for; matrix products, arithmetic and copies ran while one was open for 0% of the time, Pallas kernels for 0%

profile of v2, /device:TPU:0, one launch (start us, length us, event | category | flops | bytes accessed | tf_op | source)
XLA Modules:
  0.0 47.8 jit_solution(11843692196964591631)
XLA Ops:
  0.6 0.0 copy-start
  0.6 2.1 %copy-done = bf16[1,3,128,5120]{3,2,1,0:T(8,128)(2,1)S(1)} copy-done((bf16[1,3,128,5120]{3,2,1,0:T(8,128)(2,1)S(1)}, bf16[1,3,128,5120]{3,2,1,0:T(8,128)(2,1)}, u32[]{:S(2)}) %copy-start) | copy-done | bytes 3932184
  2.7 0.0 copy-start.1
  2.8 2.1 %copy-done.1 = bf16[1,3,128,5120]{3,2,1,0:T(8,128)(2,1)S(1)} copy-done((bf16[1,3,128,5120]{3,2,1,0:T(8,128)(2,1)S(1)}, bf16[1,3,128,5120]{3,2,1,0:T(8,128)(2,1)}, u32[]{:S(2)}) %copy-start.1) | copy-done | bytes 3932184
  4.9 0.0 copy-start.2
  4.9 1.3 %copy-done.2 = bf16[1,128,5120]{2,1,0:T(8,128)(2,1)S(1)} copy-done((bf16[1,128,5120]{2,1,0:T(8,128)(2,1)S(1)}, bf16[1,128,5120]{2,1,0:T(8,128)(2,1)}, u32[]{:S(2)}) %copy-start.2) | copy-done | bytes 1310744
  6.2 0.0 copy-start.3
  6.2 1.3 %copy-done.3 = bf16[1,5120,128]{2,1,0:T(8,128)(2,1)S(1)} copy-done((bf16[1,5120,128]{2,1,0:T(8,128)(2,1)S(1)}, bf16[1,5120,128]{2,1,0:T(8,128)(2,1)}, u32[]{:S(2)}) %copy-start.3) | copy-done | bytes 1310744
  7.5 0.0 copy-start.4
  7.5 1.1 %copy-done.4 = bf16[1,5120,64]{1,2,0:T(8,128)(2,1)S(1)} copy-done((bf16[1,5120,64]{1,2,0:T(8,128)(2,1)S(1)}, bf16[1,5120,64]{1,2,0:T(8,128)(2,1)}, u32[]{:S(2)}) %copy-start.4) | copy-done | bytes 655384
  8.6 0.0 copy-start.5
  8.6 1.1 %copy-done.5 = bf16[1,5120,64]{1,2,0:T(8,128)(2,1)S(1)} copy-done((bf16[1,5120,64]{1,2,0:T(8,128)(2,1)S(1)}, bf16[1,5120,64]{1,2,0:T(8,128)(2,1)}, u32[]{:S(2)}) %copy-start.5) | copy-done | bytes 655384
  9.7 0.0 copy-start.7
  9.7 0.8 %copy-done.7 = bf16[1,128,128]{2,1,0:T(8,128)(2,1)S(1)} copy-done((bf16[1,128,128]{2,1,0:T(8,128)(2,1)S(1)}, bf16[1,128,128]{2,1,0:T(8,128)(2,1)}, u32[]{:S(2)}) %copy-start.7) | copy-done | bytes 32792
  10.4 0.0 copy-start.8
  10.4 0.8 %copy-done.8 = bf16[1,128,128]{2,1,0:T(8,128)(2,1)S(1)} copy-done((bf16[1,128,128]{2,1,0:T(8,128)(2,1)S(1)}, bf16[1,128,128]{2,1,0:T(8,128)(2,1)}, u32[]{:S(2)}) %copy-start.8) | copy-done | bytes 32792
  11.2 0.0 copy-start.9
  11.2 0.7 %copy-done.9 = s32[3]{0:T(128)S(1)} copy-done((s32[3]{0:T(128)S(1)}, s32[3]{0:T(128)}, u32[]{:S(2)}) %copy-start.9) | copy-done | bytes 36
  11.8 0.0 copy-start.6
  11.8 0.0 copy-start.10
  11.8 7.3 %project.1 = bf16[4,4,3,16,128]{4,3,2,1,0:T(8,128)(2,1)} custom-call(s32[3]{0:T(128)S(1)} %copy-done.9, bf16[384,5120]{1,0:T(8,128)(2,1)S(1)} %bitcast.18, bf16[384,5120]{1,0:T(8,128)(2,1)S(1)} %bitcast.19, bf16[128,5120]{1,0:T(8,128)(2,1)S(1)} %bitcast.20, bf16[5120,128]{1,0:T(8,128)(2,1)S(1)} %bitcast.21, bf16[64,5120]{1,0:T(8,128)(2,1)S(1)} %bitcast.23, ...), custom_call_target="tpu_custom_call" | custom-call | flops 1509949440 | bytes 11796480 | tf_op jit(solution)/shard_map/project/pallas_call | solution.py:113
  19.2 6.3 %all-to-all-start = ((bf16[16,3,16,128]{3,2,1,0:T(8,128)(2,1)}), bf16[16,3,16,128]{3,2,1,0:T(8,128)(2,1)S(1)}, u32[]{:S(2)}, u32[]{:S(2)}) async-start(bf16[16,3,16,128]{3,2,1,0:T(8,128)(2,1)} %bitcast.11), calls=%async_computation | async-start | bytes 393216 | tf_op jit(solution)/shard_map/all_to_all | solution.py:264
  25.5 0.0 copy-done.6
  25.5 0.0 copy-done.10
  25.5 2.7 %collective-permute-start = (bf16[40,2048]{1,0:T(8,128)(2,1)S(1)}, bf16[40,2048]{1,0:T(8,128)(2,1)S(1)}, u32[]{:S(2)}, u32[]{:S(2)}) collective-permute-start(bf16[40,2048]{1,0:T(8,128)(2,1)S(1)} %payload.1.rest_0_), channel_id=1, source_target_pairs={{0,4},{4,0},{1,5},{5,1},{2,6},{6,2},{3,7},{7,3},{8,12},{12,8},{9,1... | collective-permute-start | bytes 491528 | tf_op jit(solution)/shard_map/ppermute | solution.py:245
  28.2 8.4 %collective-permute-done.rest_1_ = bf16[40,2048]{1,0:T(8,128)(2,1)S(1)} collective-permute-done((bf16[40,2048]{1,0:T(8,128)(2,1)S(1)}, bf16[40,2048]{1,0:T(8,128)(2,1)S(1)}, u32[]{:S(2)}, u32[]{:S(2)}) %collective-permute-start) | collective-permute-done | bytes 163872 | tf_op jit(solution)/shard_map/ppermute | solution.py:245
  36.6 0.0 all-to-all-done
  36.6 0.8 %combine.1 = (bf16[3,2048]{1,0:T(4,128)(2,1)}, f32[4,4,8,128]{3,2,1,0:T(8,128)S(1)}) custom-call(s32[1]{0:T(128)} %bitcast.index_ref, bf16[4,4,3,16,128]{4,3,2,1,0:T(8,128)(2,1)S(1)} %bitcast.22, bf16[40,2048]{1,0:T(8,128)(2,1)S(1)} %payload.1.rest_0_, bf16[40,2048]{1,0:T(8,128)(2,1)S(1)} %collective-permute-done.rest_1_), custom_call_target="tpu_custom_call" | custom-call | tf_op jit(solution)/shard_map/combine/pallas_call | solution.py:273
  37.4 9.6 %all_to_all.10 = f32[16,8,128]{2,1,0:T(8,128)S(1)} all-to-all(f32[16,8,128]{2,1,0:T(8,128)S(1)} %bitcast.26), channel_id=1, replica_groups=mesh['feat'=4,'hi'=2,'lo'=2,'core'=2] {'feat','lo','core'}, dimensions={0} | all-to-all | bytes 131072 | tf_op jit(solution)/shard_map/all_to_all | solution.py:289
  47.0 0.8 %score.1 = f32[3,8]{1,0:T(4,128)} custom-call(f32[4,4,8,128]{3,2,1,0:T(8,128)S(1)} %bitcast.25), custom_call_target="tpu_custom_call" | custom-call | tf_op jit(solution)/shard_map/score/pallas_call | solution.py:290
  (1 shorter events, 0.0 us)
Async XLA Ops:
  0.6 2.1 %copy-start = (bf16[1,3,128,5120]{3,2,1,0:T(8,128)(2,1)S(1)}, bf16[1,3,128,5120]{3,2,1,0:T(8,128)(2,1)}, u32[]{:S(2)}) copy-start(bf16[1,3,128,5120]{3,2,1,0:T(8,128)(2,1)} %param.11) | copy-start | bytes 11796484
  2.7 2.1 %copy-start.1 = (bf16[1,3,128,5120]{3,2,1,0:T(8,128)(2,1)S(1)}, bf16[1,3,128,5120]{3,2,1,0:T(8,128)(2,1)}, u32[]{:S(2)}) copy-start(bf16[1,3,128,5120]{3,2,1,0:T(8,128)(2,1)} %param.12) | copy-start | bytes 11796484
  4.9 1.3 %copy-start.2 = (bf16[1,128,5120]{2,1,0:T(8,128)(2,1)S(1)}, bf16[1,128,5120]{2,1,0:T(8,128)(2,1)}, u32[]{:S(2)}) copy-start(bf16[1,128,5120]{2,1,0:T(8,128)(2,1)} %param.13) | copy-start | bytes 3932164
  6.2 1.3 %copy-start.3 = (bf16[1,5120,128]{2,1,0:T(8,128)(2,1)S(1)}, bf16[1,5120,128]{2,1,0:T(8,128)(2,1)}, u32[]{:S(2)}) copy-start(bf16[1,5120,128]{2,1,0:T(8,128)(2,1)} %param.14) | copy-start | bytes 3932164
  7.5 1.1 %copy-start.4 = (bf16[1,5120,64]{1,2,0:T(8,128)(2,1)S(1)}, bf16[1,5120,64]{1,2,0:T(8,128)(2,1)}, u32[]{:S(2)}) copy-start(bf16[1,5120,64]{1,2,0:T(8,128)(2,1)} %param.15) | copy-start | bytes 1966084
  8.6 1.1 %copy-start.5 = (bf16[1,5120,64]{1,2,0:T(8,128)(2,1)S(1)}, bf16[1,5120,64]{1,2,0:T(8,128)(2,1)}, u32[]{:S(2)}) copy-start(bf16[1,5120,64]{1,2,0:T(8,128)(2,1)} %param.16) | copy-start | bytes 1966084
  9.7 0.8 %copy-start.7 = (bf16[1,128,128]{2,1,0:T(8,128)(2,1)S(1)}, bf16[1,128,128]{2,1,0:T(8,128)(2,1)}, u32[]{:S(2)}) copy-start(bf16[1,128,128]{2,1,0:T(8,128)(2,1)} %param.17) | copy-start | bytes 98308
  10.4 0.8 %copy-start.8 = (bf16[1,128,128]{2,1,0:T(8,128)(2,1)S(1)}, bf16[1,128,128]{2,1,0:T(8,128)(2,1)}, u32[]{:S(2)}) copy-start(bf16[1,128,128]{2,1,0:T(8,128)(2,1)} %param.18) | copy-start | bytes 98308
  11.2 0.7 %copy-start.9 = (s32[3]{0:T(128)S(1)}, s32[3]{0:T(128)}, u32[]{:S(2)}) copy-start(s32[3]{0:T(128)} %counts_ref.1) | copy-start | bytes 40
  11.8 13.6 %copy-start.6 = (bf16[32,2048]{1,0:T(8,128)(2,1)S(1)}, bf16[32,2048]{1,0:T(8,128)(2,1)}, u32[]{:S(2)}) copy-start(bf16[32,2048]{1,0:T(8,128)(2,1)} %val_ref.1) | copy-start | bytes 393220
  11.8 13.6 %copy-start.10 = (s32[32,1]{0,1:T(1,128)S(1)}, s32[32,1]{0,1:T(1,128)}, u32[]{:S(2)}) copy-start(s32[32,1]{0,1:T(1,128)} %param.21) | copy-start | bytes 388
  19.2 17.4 %all-to-all-start = ((bf16[16,3,16,128]{3,2,1,0:T(8,128)(2,1)}), bf16[16,3,16,128]{3,2,1,0:T(8,128)(2,1)S(1)}, u32[]{:S(2)}, u32[]{:S(2)}) async-start(bf16[16,3,16,128]{3,2,1,0:T(8,128)(2,1)} %bitcast.11), calls=%async_computation | async-start | bytes 393216 | tf_op jit(solution)/shard_map/all_to_all | solution.py:264
  25.5 11.0 %collective-permute-start = (bf16[40,2048]{1,0:T(8,128)(2,1)S(1)}, bf16[40,2048]{1,0:T(8,128)(2,1)S(1)}, u32[]{:S(2)}, u32[]{:S(2)}) collective-permute-start(bf16[40,2048]{1,0:T(8,128)(2,1)S(1)} %payload.1.rest_0_), channel_id=1, source_target_pairs={{0,4},{4,0},{1,5},{5,1},{2,6},{6,2},{3,7},{7,3},{8,12},{12,8},{9,1... | collective-permute-start | bytes 491528 | tf_op jit(solution)/shard_map/ppermute | solution.py:245

commit v3 on v2

--- a/solution.py
+++ b/solution.py
@@ -13,6 +13,8 @@
 DOMAINS = 8
 LANES = 128
 SUBLANES = 8
+CHUNKS = 4
+PROJECT_VMEM = 67_043_328 - 614_400
 
 FAR = ("hi",)
 NEAR = ("lo", "core")
@@ -40,109 +42,151 @@
     return (value + unit - 1) // unit * unit
 
 
-def payload_kernel(val_ref, domain_ref, out_ref):
-    rows = val_ref.shape[0]
-    out_ref[:rows, :] = val_ref[...]
-    out_ref[rows:, :] = jnp.zeros_like(out_ref[rows:, :])
-    ids = jnp.broadcast_to(domain_ref[...].astype(jnp.float32), (SUBLANES, rows))
-    out_ref[rows : rows + SUBLANES, :rows] = ids.astype(jnp.bfloat16)
-
-
 def project_kernel(
-    steps,
     counts_ref,
+    x_hbm,
+    g_hbm,
+    a_hbm,
+    b_hbm,
+    of_hbm,
+    if_hbm,
+    rb_hbm,
+    ra_hbm,
+    out_ref,
     x_ref,
     g_ref,
-    a_ref,
+    wx_ref,
     b_ref,
     of_ref,
-    if_ref,
     rb_ref,
     ra_ref,
-    out_ref,
     acc_x,
-    acc_b,
-    acc_o,
+    acc_g,
+    x_sems,
+    g_sems,
+    sems,
 ):
-    step = pl.program_id(0)
-    rank = a_ref.shape[0]
-    rows = of_ref.shape[0]
     feat_size, copies, examples, part, _ = out_ref.shape
-    seq = acc_x.shape[0] // examples
-
-    @pl.when(step == 0)
-    def _():
-        acc_x[...] = jnp.zeros_like(acc_x)
-        acc_b[...] = jnp.zeros_like(acc_b)
-        acc_o[...] = jnp.zeros_like(acc_o)
-
-    weights_x = jnp.concatenate([a_ref[...], if_ref[...]], axis=0)
-    acc_x[...] += dot32(x_ref[...], weights_x, NT)
-    acc_b[...] += dot32(g_ref[...], b_ref[...], NN)
-    acc_o[...] += dot32(g_ref[...], of_ref[...], NT)
-
-    @pl.when(step == steps - 1)
-    def _():
-        hidden = acc_x[:, :rank].astype(jnp.bfloat16)
-        back = acc_b[...].astype(jnp.bfloat16)
+    chunks, tokens, chunk = x_ref.shape
+    seq = tokens // examples
+    rank = a_hbm.shape[0]
+    rows = of_hbm.shape[0]
+
+    def x_moves(c):
+        span = pl.ds(pl.multiple_of(c * chunk, LANES), chunk)
+        return (
+            pltpu.make_async_copy(x_hbm.at[:, span], x_ref.at[c], x_sems.at[c, 0]),
+            pltpu.make_async_copy(a_hbm.at[:, span], wx_ref.at[c, :rank], x_sems.at[c, 1]),
+            pltpu.make_async_copy(if_hbm.at[:, span], wx_ref.at[c, rank:], x_sems.at[c, 2]),
+        )
+
+    def g_moves(c):
+        span = pl.ds(pl.multiple_of(c * chunk, LANES), chunk)
+        return (
+            pltpu.make_async_copy(g_hbm.at[:, span], g_ref.at[c], g_sems.at[c, 0]),
+            pltpu.make_async_copy(b_hbm.at[span, :], b_ref.at[c], g_sems.at[c, 1]),
+            pltpu.make_async_copy(of_hbm.at[:, span], of_ref.at[c], g_sems.at[c, 2]),
+        )
+
+    small = [
+        pltpu.make_async_copy(rb_hbm, rb_ref, sems.at[0]),
+        pltpu.make_async_copy(ra_hbm, ra_ref, sems.at[1]),
+    ]
+
+    @pl.loop(0, chunks)
+    def _(c):
+        for move in x_moves(c):
+            move.start()
+
+    for move in small:
+        move.start()
+
+    @pl.loop(0, chunks)
+    def _(c):
+        for move in g_moves(c):
+            move.start()
+
+    acc_x[...] = jnp.zeros_like(acc_x)
+    acc_g[...] = jnp.zeros_like(acc_g)
+
+    @pl.loop(0, chunks)
+    def _(c):
+        for move in x_moves(c):
+            move.wait()
+        acc_x[...] += dot32(x_ref[c], wx_ref[c], NT)
+
+    for move in small:
+        move.wait()
+
+    @pl.loop(0, chunks)
+    def _(c):
+        for move in g_moves(c):
+            move.wait()
+        weights = jnp.concatenate([b_ref[c], of_ref[c].T], axis=1)
+        acc_g[...] += dot32(g_ref[c], weights, NN)
+
+    place = lax.broadcasted_iota(jnp.int32, (seq, rows), 0)
+
+    @pl.loop(0, examples)
+    def _(e):
+        span = pl.ds(pl.multiple_of(e * seq, seq), seq)
+        live = place < counts_ref[e]
+        hidden = acc_x[span, :rank].astype(jnp.bfloat16)
+        back = acc_g[span, :rank].astype(jnp.bfloat16)
         hidden_rank = dot32(hidden, rb_ref[...], NN).astype(jnp.bfloat16)
         back_rank = dot32(back, ra_ref[...], NN).astype(jnp.bfloat16)
-        place = lax.broadcasted_iota(jnp.int32, (seq, rows), 0)
-        for e in range(examples):
-            span = slice(e * seq, (e + 1) * seq)
-            live = place < counts_ref[e]
-            gp = jnp.where(live, acc_o[span, :], 0.0).astype(jnp.bfloat16)
-            ip = jnp.where(live, acc_x[span, rank:], 0.0).astype(jnp.bfloat16)
-            term = dot32(gp, hidden_rank[span], TN) + dot32(ip, back_rank[span], TN)
-            term = (term / counts_ref[e].astype(jnp.float32)).astype(jnp.bfloat16)
-            for f in range(feat_size):
-                for q in range(copies):
-                    out_ref[f, q, e] = term[f * part : (f + 1) * part]
-
-
-def project(counts, x, g, a, b, of_t, if_t, rb, ra, feat_size, copies, examples):
+        gp = jnp.where(live, acc_g[span, rank:], 0.0).astype(jnp.bfloat16)
+        ip = jnp.where(live, acc_x[span, rank:], 0.0).astype(jnp.bfloat16)
+        term = dot32(gp, hidden_rank, TN) + dot32(ip, back_rank, TN)
+        term = (term / counts_ref[e].astype(jnp.float32)).astype(jnp.bfloat16)
+        for f in range(feat_size):
+            for q in range(copies):
+                out_ref[f, q, e] = term[f * part : (f + 1) * part]
+
+
+def project(counts, arrays, feat_size, copies, examples):
+    x, _, a, _, of_t, _, rb, _ = arrays
     tokens, width = x.shape
-    rank = a.shape[0]
-    rows = of_t.shape[0]
-    cols = rb.shape[1]
-    steps = 10
-    kb = width // steps
-    part = rows // feat_size
-    whole = lambda shape: pl.BlockSpec(shape, lambda k: (0,) * len(shape))
-    out = (feat_size, copies, examples, part, cols)
+    rank, rows = a.shape[0], of_t.shape[0]
+    chunk = width // CHUNKS
+    out = (feat_size, copies, examples, rows // feat_size, rb.shape[1])
+    hbm = pl.BlockSpec(memory_space=pltpu.HBM)
+    vmem = pl.BlockSpec(memory_space=pltpu.VMEM)
+    low = [
+        (CHUNKS, tokens, chunk),
+        (CHUNKS, tokens, chunk),
+        (CHUNKS, rank + rows, chunk),
+        (CHUNKS, chunk, rank),
+        (CHUNKS, rows, chunk),
+        rb.shape,
+        rb.shape,
+    ]
     return pl.pallas_call(
-        functools.partial(project_kernel, steps),
-        grid=(steps,),
-        in_specs=[
-            pl.BlockSpec(memory_space=pltpu.SMEM),
-            pl.BlockSpec((tokens, kb), lambda k: (0, k)),
-            pl.BlockSpec((tokens, kb), lambda k: (0, k)),
-            pl.BlockSpec((rank, kb), lambda k: (0, k)),
-            pl.BlockSpec((kb, rank), lambda k: (k, 0)),
-            pl.BlockSpec((rows, kb), lambda k: (0, k)),
-            pl.BlockSpec((rows, kb), lambda k: (0, k)),
-            whole(rb.shape),
-            whole(ra.shape),
-        ],
-        out_specs=whole(out),
+        project_kernel,
+        in_specs=[pl.BlockSpec(memory_space=pltpu.SMEM)] + [hbm] * len(arrays),
+        out_specs=vmem,
         out_shape=jax.ShapeDtypeStruct(out, jnp.bfloat16),
-        scratch_shapes=[
+        scratch_shapes=[pltpu.VMEM(shape, jnp.bfloat16) for shape in low]
+        + [
             pltpu.VMEM((tokens, rank + rows), jnp.float32),
-            pltpu.VMEM((tokens, rank), jnp.float32),
-            pltpu.VMEM((tokens, rows), jnp.float32),
+            pltpu.VMEM((tokens, rank + rows), jnp.float32),
+            pltpu.SemaphoreType.DMA((CHUNKS, 3)),
+            pltpu.SemaphoreType.DMA((CHUNKS, 3)),
+            pltpu.SemaphoreType.DMA((2,)),
         ],
         cost_estimate=pl.CostEstimate(
             flops=4 * tokens * width * (rank + rows),
             bytes_accessed=2 * (2 * tokens + 2 * rank + 2 * rows) * width,
             transcendentals=0,
         ),
-        compiler_params=limit(16),
+        compiler_params=pltpu.CompilerParams(vmem_limit_bytes=PROJECT_VMEM),
         name="project",
-    )(counts, x, g, a, b, of_t, if_t, rb, ra)
-
-
-def combine_kernel(rows, index_ref, parts_ref, *rest):
-    pieces = rest[:-4]
+    )(counts, *arrays)
+
+
+def combine_kernel(index_ref, parts_ref, *rest):
+    pieces = rest[: (len(rest) - 4) // 2]
+    domains = rest[len(pieces) : -4]
     feat_ref, pack_ref, summed, flat = rest[-4:]
     feat_size, copies, examples, part, cols = parts_ref.shape
     width = part * cols
@@ -160,17 +204,15 @@
     features = flat[...].astype(jnp.bfloat16)
     rounded = features.astype(jnp.float32)
     norm = jnp.sum(rounded * rounded, axis=1, keepdims=True)
-    count = len(pieces) * rows
-    vals = jnp.concatenate([ref[:rows, :] for ref in pieces], axis=0)
+    vals = jnp.concatenate([ref[...] for ref in pieces], axis=0)
+    count = vals.shape[0]
     inner = dot32(features, vals, NT)
     squares = jnp.zeros((count, LANES), jnp.float32)
     for c in range(0, width, LANES):
         piece = vals[:, c : c + LANES].astype(jnp.float32)
         squares = squares + piece * piece
     val_norm = dot32(jnp.ones((SUBLANES, LANES), jnp.float32), squares, NT, HIGHEST)
-    ids = jnp.concatenate(
-        [ref[rows : rows + SUBLANES, :rows].astype(jnp.float32) for ref in pieces], axis=1
-    )
+    ids = jnp.concatenate([ref[...].astype(jnp.float32) for ref in domains], axis=1)
     pack_ref[...] = jnp.full(pack_ref.shape, -1.0, jnp.float32)
     lanes = pack_ref.shape[-1]
     for q in range(copies):
@@ -184,7 +226,7 @@
 
 
 def score_kernel(count, scale, packs_ref, out_ref):
-    feat_size, copies, _, lanes = packs_ref.shape
+    feat_size, copies, _, _ = packs_ref.shape
     examples = out_ref.shape[0]
     total = packs_ref[0]
     for f in range(1, feat_size):
@@ -233,19 +275,13 @@
     copies = axis_count(sizes, NEAR)
     far_size = axis_count(sizes, FAR)
 
-    payload = pl.pallas_call(
-        payload_kernel,
-        out_shape=jax.ShapeDtypeStruct((val_rows + SUBLANES, val_cols), jnp.bfloat16),
-        compiler_params=limit(4),
-        name="payload",
-    )(val_grads, val_domain.T)
-    pieces = [payload]
+    vals, domains = [val_grads], [val_domain.T]
     for s in range(1, far_size):
         pairs = [(i, (i + s) % far_size) for i in range(far_size)]
-        pieces.append(lax.ppermute(payload, FAR, pairs))
-
-    parts = project(
-        token_counts,
+        vals.append(lax.ppermute(vals[0], FAR, pairs))
+        domains.append(lax.ppermute(domains[0], FAR, pairs))
+
+    arrays = (
         layer_inputs.reshape(examples * seq_len, width),
         output_grads.reshape(examples * seq_len, width),
         adapter_a[0],
@@ -254,10 +290,8 @@
         in_factor[0].T,
         rank_factor_b[0],
         rank_factor_a[0],
-        feat_size,
-        copies,
-        examples,
     )
+    parts = project(token_counts, arrays, feat_size, copies, examples)
     group = ("feat",) + NEAR
     members = feat_size * copies
     flat_parts = parts.reshape((members,) + parts.shape[2:])
@@ -271,8 +305,8 @@
     smem = pl.BlockSpec(memory_space=pltpu.SMEM)
     vmem = pl.BlockSpec(memory_space=pltpu.VMEM)
     train_features, packs = pl.pallas_call(
-        functools.partial(combine_kernel, val_rows),
-        in_specs=[smem] + [vmem] * (1 + far_size),
+        combine_kernel,
+        in_specs=[smem] + [vmem] * (1 + 2 * far_size),
         out_shape=[
             jax.ShapeDtypeStruct((examples, val_cols), jnp.bfloat16),
             jax.ShapeDtypeStruct((feat_size, copies, block_rows, lanes), jnp.float32),
@@ -283,7 +317,7 @@
         ],
         compiler_params=limit(8),
         name="combine",
-    )(index, got, *pieces)
+    )(index, got, *vals, *domains)
 
     flat_packs = packs.reshape((members,) + packs.shape[2:])
     returned = lax.all_to_all(flat_packs, group, 0, 0, tiled=True).reshape(packs.shape)

time: 48.4 us -> 36 us (0.74)
  local copies, waits for them, and re-layouts: 11.2 us -> 0.01 us
  waiting for transfers between devices: 8.38 us -> 6.82 us
    unnamed x22 -> x4, local copies, waits for them, and re-layouts: 11.2 us -> 0.01 us
    ppermute x1 -> x2, waiting for transfers between devices: 8.38 us -> 4.14 us  [the longest x1 4.13 us: local(): domains.append(lax.ppermute(domains[0], FAR, pairs))]
    all_to_all x1, waiting for transfers between devices: 0.01 us -> 2.68 us  [local(): lax.all_to_all(flat_parts, group, 0, 0, tiled=True).reshape(parts.shape)]
    ppermute x1 -> x2, starting transfers between devices: 2.66 us -> 2.99 us  [the longest x1 2.65 us: local(): vals.append(lax.ppermute(vals[0], FAR, pairs))]
    pallas_call x3 -> x2, Pallas kernels: 8.15 us -> 8.43 us  [the longest x1 7.6 us: project(): pl.pallas_call(project_kernel, in_specs=[pl.BlockSpec(memory_space=pltpu....]
  transfers between devices with their start and end apart: 2 -> 3, of which waited for: 1 -> 2; matrix products, arithmetic and copies ran while one was open for 0% -> 0% of each run, Pallas kernels for 0% -> 0%
where the time goes in v3:
time: 36 us; the launch traced here: 35.7 us
  blocking collectives  9.67 us (27%)
  starting transfers between devices  9.33 us (26%)
  Pallas kernels  9.21 us (26%)
  waiting for transfers between devices  6.82 us (19%)
  between operations  0.68 us (2%)
    all_to_all x1, blocking collectives, local(): lax.all_to_all(flat_packs, group, 0, 0, tiled=True).reshape(packs.shape)  9.67 us
    pallas_call x1, Pallas kernels, project(): pl.pallas_call(project_kernel, in_specs=[pl.BlockSpec(memory_space=pltpu....  7.6 us
    all_to_all x1, starting transfers between devices, local(): lax.all_to_all(flat_parts, group, 0, 0, tiled=True).reshape(parts.shape)  6.34 us
    ppermute x1, waiting for transfers between devices, local(): domains.append(lax.ppermute(domains[0], FAR, pairs))  4.13 us
    all_to_all x1, waiting for transfers between devices, local(): lax.all_to_all(flat_parts, group, 0, 0, tiled=True).reshape(parts.shape)  2.68 us
    ppermute x1, starting transfers between devices, local(): vals.append(lax.ppermute(vals[0], FAR, pairs))  2.65 us
    pallas_call x1, Pallas kernels, local(): pl.pallas_call(combine_kernel, in_specs=[smem] + [vmem] * (1 + 2 * far_si...  0.82 us
    pallas_call x1, Pallas kernels, local(): pl.pallas_call(functools.partial(score_kernel, count, math.sqrt(PROJ)), o...  0.79 us
  transfers between devices with their start and end apart: 3, of which 2 were waited for; matrix products, arithmetic and copies ran while one was open for 0% of the time, Pallas kernels for 0%

profile of v3, /device:TPU:0, one launch (start us, length us, event | category | flops | bytes accessed | tf_op | source)
XLA Modules:
  0.0 35.7 jit_solution(2794709332299831538)
XLA Ops:
  0.6 0.0 copy-start
  0.6 0.0 copy-start.1
  0.7 7.6 %project.1 = bf16[4,4,3,16,128]{4,3,2,1,0:T(8,128)(2,1)} custom-call(s32[3]{0:T(128)} %counts_ref.1, bf16[384,5120]{1,0:T(8,128)(2,1)} %bitcast.23, bf16[384,5120]{1,0:T(8,128)(2,1)} %bitcast.24, bf16[128,5120]{1,0:T(8,128)(2,1)} %bitcast.25, bf16[5120,128]{1,0:T(8,128)(2,1)} %bitcast.26, bf16[64,5120]{1,0:T(8,128)(2,1)} %bitcast.28, ...), custom_call_target="tpu_custom_call" | custom-call | flops 1509949440 | bytes 11796480 | tf_op jit(solution)/shard_map/project/pallas_call | solution.py:164
  8.3 6.3 %all-to-all-start = ((bf16[16,3,16,128]{3,2,1,0:T(8,128)(2,1)}), bf16[16,3,16,128]{3,2,1,0:T(8,128)(2,1)S(1)}, u32[]{:S(2)}, u32[]{:S(2)}) async-start(bf16[16,3,16,128]{3,2,1,0:T(8,128)(2,1)} %bitcast.27), calls=%async_computation | async-start | bytes 393216 | tf_op jit(solution)/shard_map/all_to_all | solution.py:298
  14.6 0.0 copy-done
  14.6 2.6 %collective-permute-start = (bf16[32,2048]{1,0:T(8,128)(2,1)S(1)}, bf16[32,2048]{1,0:T(8,128)(2,1)S(1)}, u32[]{:S(2)}, u32[]{:S(2)}) collective-permute-start(bf16[32,2048]{1,0:T(8,128)(2,1)S(1)} %copy-done), channel_id=1, source_target_pairs={{0,4},{4,0},{1,5},{5,1},{2,6},{6,2},{3,7},{7,3},{8,12},{12,8},{9,1... | collective-permute-start | bytes 393224 | tf_op jit(solution)/shard_map/ppermute | solution.py:281
  17.3 0.0 copy-done.1
  17.3 0.3 collective-permute-start.1
  17.6 4.1 %collective-permute-done.1.rest_3_ = s32[1,32]{1,0:T(1,128)S(1)} collective-permute-done((s32[1,32]{1,0:T(1,128)S(1)}, s32[1,32]{1,0:T(1,128)S(1)}, u32[]{:S(2)}, u32[]{:S(2)}) %collective-permute-start.1) | collective-permute-done | bytes 160 | tf_op jit(solution)/shard_map/ppermute | solution.py:282
  21.7 0.0 collective-permute-done.rest_1_
  21.8 2.7 %all-to-all-done = bf16[16,3,16,128]{3,2,1,0:T(8,128)(2,1)S(1)} async-done(((bf16[16,3,16,128]{3,2,1,0:T(8,128)(2,1)}), bf16[16,3,16,128]{3,2,1,0:T(8,128)(2,1)S(1)}, u32[]{:S(2)}, u32[]{:S(2)}) %all-to-all-start) | async-done | bytes 196640 | tf_op jit(solution)/shard_map/all_to_all | solution.py:298
  24.4 0.8 %combine.1 = (bf16[3,2048]{1,0:T(4,128)(2,1)}, f32[4,4,8,128]{3,2,1,0:T(8,128)S(1)}) custom-call(s32[1]{0:T(128)} %bitcast.index_ref, bf16[4,4,3,16,128]{4,3,2,1,0:T(8,128)(2,1)S(1)} %bitcast.18, bf16[32,2048]{1,0:T(8,128)(2,1)S(1)} %copy-done, bf16[32,2048]{1,0:T(8,128)(2,1)S(1)} %collective-permute-done.rest_1_, s32[1,32]{1,0:T(1,128)S(1)} %bitcast.22, ...), custom_call_target="tpu_custom_call" | custom-call | tf_op jit(solution)/shard_map/combine/pallas_call | solution.py:307
  25.3 9.7 %all_to_all.10 = f32[16,8,128]{2,1,0:T(8,128)S(1)} all-to-all(f32[16,8,128]{2,1,0:T(8,128)S(1)} %bitcast.20), channel_id=1, replica_groups=mesh['feat'=4,'hi'=2,'lo'=2,'core'=2] {'feat','lo','core'}, dimensions={0} | all-to-all | bytes 131072 | tf_op jit(solution)/shard_map/all_to_all | solution.py:323
  34.9 0.8 %score.1 = f32[3,8]{1,0:T(4,128)} custom-call(f32[4,4,8,128]{3,2,1,0:T(8,128)S(1)} %bitcast.19), custom_call_target="tpu_custom_call" | custom-call | tf_op jit(solution)/shard_map/score/pallas_call | solution.py:324
Async XLA Ops:
  0.6 14.0 %copy-start = (bf16[32,2048]{1,0:T(8,128)(2,1)S(1)}, bf16[32,2048]{1,0:T(8,128)(2,1)}, u32[]{:S(2)}) copy-start(bf16[32,2048]{1,0:T(8,128)(2,1)} %rest_0_.1) | copy-start | bytes 393220
  0.6 16.6 %copy-start.1 = (s32[32,1]{0,1:T(1,128)S(1)}, s32[32,1]{0,1:T(1,128)}, u32[]{:S(2)}) copy-start(s32[32,1]{0,1:T(1,128)} %param.21) | copy-start | bytes 388
  8.3 16.2 %all-to-all-start = ((bf16[16,3,16,128]{3,2,1,0:T(8,128)(2,1)}), bf16[16,3,16,128]{3,2,1,0:T(8,128)(2,1)S(1)}, u32[]{:S(2)}, u32[]{:S(2)}) async-start(bf16[16,3,16,128]{3,2,1,0:T(8,128)(2,1)} %bitcast.27), calls=%async_computation | async-start | bytes 393216 | tf_op jit(solution)/shard_map/all_to_all | solution.py:298
  14.6 7.1 %collective-permute-start = (bf16[32,2048]{1,0:T(8,128)(2,1)S(1)}, bf16[32,2048]{1,0:T(8,128)(2,1)S(1)}, u32[]{:S(2)}, u32[]{:S(2)}) collective-permute-start(bf16[32,2048]{1,0:T(8,128)(2,1)S(1)} %copy-done), channel_id=1, source_target_pairs={{0,4},{4,0},{1,5},{5,1},{2,6},{6,2},{3,7},{7,3},{8,12},{12,8},{9,1... | collective-permute-start | bytes 393224 | tf_op jit(solution)/shard_map/ppermute | solution.py:281
  17.3 4.5 %collective-permute-start.1 = (s32[1,32]{1,0:T(1,128)S(1)}, s32[1,32]{1,0:T(1,128)S(1)}, u32[]{:S(2)}, u32[]{:S(2)}) collective-permute-start(s32[1,32]{1,0:T(1,128)S(1)} %bitcast.21), channel_id=1, source_target_pairs={{0,4},{4,0},{1,5},{5,1},{2,6},{6,2},{3,7},{7,3},{8,12},{12,8},{9,1... | collective-permute-start | bytes 392 | tf_op jit(solution)/shard_map/ppermute | solution.py:282

commit v4 on v3

--- a/solution.py
+++ b/solution.py
@@ -14,13 +14,14 @@
 LANES = 128
 SUBLANES = 8
 CHUNKS = 4
-PROJECT_VMEM = 67_043_328 - 614_400
-
-FAR = ("hi",)
-NEAR = ("lo", "core")
+PROJECT_VMEM = 67_043_328 - 1_300_000
+
+FAR = ("hi", "lo")
+NEAR = ("core",)
 DP = ("hi", "lo", "core")
 
 norm_eps = 1e-06
+
 
 NT = (((1,), (1,)), ((), ()))
 NN = (((1,), (0,)), ((), ()))
@@ -40,6 +41,21 @@
 
 def round_up(value, unit):
     return (value + unit - 1) // unit * unit
+
+
+def payload_kernel(val_hbm, domain_hbm, out_ref, domain_ref, sems):
+    rows = val_hbm.shape[0]
+    moves = [
+        pltpu.make_async_copy(domain_hbm, domain_ref, sems.at[0]),
+        pltpu.make_async_copy(val_hbm, out_ref.at[:rows, :], sems.at[1]),
+    ]
+    for move in moves:
+        move.start()
+    out_ref[rows:, :] = jnp.zeros_like(out_ref[rows:, :])
+    moves[0].wait()
+    ids = jnp.broadcast_to(domain_ref[...].astype(jnp.float32), (SUBLANES, rows))
+    out_ref[rows:, :rows] = ids.astype(jnp.bfloat16)
+    moves[1].wait()
 
 
 def project_kernel(
@@ -165,7 +181,7 @@
         project_kernel,
         in_specs=[pl.BlockSpec(memory_space=pltpu.SMEM)] + [hbm] * len(arrays),
         out_specs=vmem,
-        out_shape=jax.ShapeDtypeStruct(out, jnp.bfloat16),
+        out_shape=pltpu.VMEM(out, jnp.bfloat16),
         scratch_shapes=[pltpu.VMEM(shape, jnp.bfloat16) for shape in low]
         + [
             pltpu.VMEM((tokens, rank + rows), jnp.float32),
@@ -184,9 +200,8 @@
     )(counts, *arrays)
 
 
-def combine_kernel(index_ref, parts_ref, *rest):
-    pieces = rest[: (len(rest) - 4) // 2]
-    domains = rest[len(pieces) : -4]
+def combine_kernel(rows, index_ref, parts_ref, *rest):
+    pieces = rest[:-4]
     feat_ref, pack_ref, summed, flat = rest[-4:]
     feat_size, copies, examples, part, cols = parts_ref.shape
     width = part * cols
@@ -204,7 +219,7 @@
     features = flat[...].astype(jnp.bfloat16)
     rounded = features.astype(jnp.float32)
     norm = jnp.sum(rounded * rounded, axis=1, keepdims=True)
-    vals = jnp.concatenate([ref[...] for ref in pieces], axis=0)
+    vals = jnp.concatenate([ref[:rows, :] for ref in pieces], axis=0)
     count = vals.shape[0]
     inner = dot32(features, vals, NT)
     squares = jnp.zeros((count, LANES), jnp.float32)
@@ -212,7 +227,9 @@
         piece = vals[:, c : c + LANES].astype(jnp.float32)
         squares = squares + piece * piece
     val_norm = dot32(jnp.ones((SUBLANES, LANES), jnp.float32), squares, NT, HIGHEST)
-    ids = jnp.concatenate([ref[...].astype(jnp.float32) for ref in domains], axis=1)
+    ids = jnp.concatenate(
+        [ref[rows : rows + SUBLANES, :rows].astype(jnp.float32) for ref in pieces], axis=1
+    )
     pack_ref[...] = jnp.full(pack_ref.shape, -1.0, jnp.float32)
     lanes = pack_ref.shape[-1]
     for q in range(copies):
@@ -275,11 +292,22 @@
     copies = axis_count(sizes, NEAR)
     far_size = axis_count(sizes, FAR)
 
-    vals, domains = [val_grads], [val_domain.T]
+    payload = pl.pallas_call(
+        payload_kernel,
+        in_specs=[pl.BlockSpec(memory_space=pltpu.HBM)] * 2,
+        out_specs=pl.BlockSpec(memory_space=pltpu.VMEM),
+        out_shape=pltpu.VMEM((val_rows + SUBLANES, val_cols), jnp.bfloat16),
+        scratch_shapes=[
+            pltpu.VMEM((1, val_rows), jnp.int32),
+            pltpu.SemaphoreType.DMA((2,)),
+        ],
+        compiler_params=pltpu.CompilerParams(vmem_limit_bytes=PROJECT_VMEM),
+        name="payload",
+    )(val_grads, val_domain.T)
+    pieces = [payload]
     for s in range(1, far_size):
         pairs = [(i, (i + s) % far_size) for i in range(far_size)]
-        vals.append(lax.ppermute(vals[0], FAR, pairs))
-        domains.append(lax.ppermute(domains[0], FAR, pairs))
+        pieces.append(lax.ppermute(payload, FAR, pairs))
 
     arrays = (
         layer_inputs.reshape(examples * seq_len, width),
@@ -294,6 +322,8 @@
     parts = project(token_counts, arrays, feat_size, copies, examples)
     group = ("feat",) + NEAR
     members = feat_size * copies
+    index = lax.axis_index(NEAR).astype(jnp.int32).reshape(1)
+    parts, index = lax.optimization_barrier((parts, index))
     flat_parts = parts.reshape((members,) + parts.shape[2:])
     got = lax.all_to_all(flat_parts, group, 0, 0, tiled=True).reshape(parts.shape)
 
@@ -301,12 +331,11 @@
     lanes = round_up(count, LANES)
     block_rows = round_up(2 * examples + 2, SUBLANES)
     part, cols = parts.shape[3:]
-    index = lax.axis_index(NEAR).astype(jnp.int32).reshape(1)
     smem = pl.BlockSpec(memory_space=pltpu.SMEM)
     vmem = pl.BlockSpec(memory_space=pltpu.VMEM)
     train_features, packs = pl.pallas_call(
-        combine_kernel,
-        in_specs=[smem] + [vmem] * (1 + 2 * far_size),
+        functools.partial(combine_kernel, val_rows),
+        in_specs=[smem] + [vmem] * (1 + far_size),
         out_shape=[
             jax.ShapeDtypeStruct((examples, val_cols), jnp.bfloat16),
             jax.ShapeDtypeStruct((feat_size, copies, block_rows, lanes), jnp.float32),
@@ -317,7 +346,7 @@
         ],
         compiler_params=limit(8),
         name="combine",
-    )(index, got, *vals, *domains)
+    )(index, got, *pieces)
 
     flat_packs = packs.reshape((members,) + packs.shape[2:])
     returned = lax.all_to_all(flat_packs, group, 0, 0, tiled=True).reshape(packs.shape)

time: 36 us -> 32.4 us (0.90)
  waiting for transfers between devices: 6.82 us -> 0.01 us
  blocking collectives: 9.67 us -> 15.9 us
  starting transfers between devices: 9.33 us -> 6.14 us
    all_to_all x0 -> x1, blocking collectives: none -> 8.71 us  [local(): lax.all_to_all(flat_parts, group, 0, 0, tiled=True).reshape(parts.shape)]
    all_to_all x1 -> x0, starting transfers between devices: 6.34 us -> none  [local(): lax.all_to_all(flat_parts, group, 0, 0, tiled=True).reshape(parts.shape)]
    ppermute x2 -> x3, waiting for transfers between devices: 4.14 us -> 0.01 us  [local(): pieces.append(lax.ppermute(payload, FAR, pairs))]
    ppermute x2 -> x3, starting transfers between devices: 2.99 us -> 6.14 us  [local(): pieces.append(lax.ppermute(payload, FAR, pairs))]
    all_to_all x1 -> x0, waiting for transfers between devices: 2.68 us -> none  [local(): lax.all_to_all(flat_parts, group, 0, 0, tiled=True).reshape(parts.shape)]
    all_to_all x1, blocking collectives: 9.67 us -> 7.2 us  [local(): lax.all_to_all(flat_packs, group, 0, 0, tiled=True).reshape(packs.shape)]
    pallas_call x1 -> x2, Pallas kernels: 0.82 us -> 1.86 us  [the longest x1 0.94 us: local(): pl.pallas_call(payload_kernel, in_specs=[pl.BlockSpec(memory_space=pltpu....]
    pallas_call x1, Pallas kernels: 7.6 us -> 6.81 us  [project(): pl.pallas_call(project_kernel, in_specs=[pl.BlockSpec(memory_space=pltpu....]
  transfers between devices with their start and end apart: 3 -> 3, of which waited for: 2 -> 0; matrix products, arithmetic and copies ran while one was open for 0% -> 0% of each run, Pallas kernels for 0% -> 21%
where the time goes in v4:
time: 32.4 us; the launch traced here: 32.1 us
  blocking collectives  15.9 us (49%)
  Pallas kernels  9.42 us (29%)
  starting transfers between devices  6.14 us (19%)
  between operations  0.65 us (2%)
    all_to_all x1, blocking collectives, local(): lax.all_to_all(flat_parts, group, 0, 0, tiled=True).reshape(parts.shape)  8.71 us
    all_to_all x1, blocking collectives, local(): lax.all_to_all(flat_packs, group, 0, 0, tiled=True).reshape(packs.shape)  7.2 us
    pallas_call x1, Pallas kernels, project(): pl.pallas_call(project_kernel, in_specs=[pl.BlockSpec(memory_space=pltpu....  6.81 us
    ppermute x3, starting transfers between devices, local(): pieces.append(lax.ppermute(payload, FAR, pairs))  6.14 us
    pallas_call x1, Pallas kernels, local(): pl.pallas_call(payload_kernel, in_specs=[pl.BlockSpec(memory_space=pltpu....  0.94 us
    pallas_call x1, Pallas kernels, local(): pl.pallas_call(functools.partial(combine_kernel, val_rows), in_specs=[sme...  0.92 us
    pallas_call x1, Pallas kernels, local(): pl.pallas_call(functools.partial(score_kernel, count, math.sqrt(PROJ)), o...  0.75 us
  transfers between devices with their start and end apart: 3, of which 0 were waited for; matrix products, arithmetic and copies ran while one was open for 0% of the time, Pallas kernels for 21%

profile of v4, /device:TPU:0, one launch (start us, length us, event | category | flops | bytes accessed | tf_op | source)
XLA Modules:
  0.0 32.1 jit_solution(2684971228210132420)
XLA Ops:
  0.6 0.9 %payload.1.rest_0_ = bf16[40,2048]{1,0:T(8,128)(2,1)S(1)} custom-call(bf16[32,2048]{1,0:T(8,128)(2,1)} %val_hbm.1, s32[1,32]{1,0:T(1,128)} %bitcast.30), custom_call_target="tpu_custom_call" | custom-call | tf_op jit(solution)/shard_map/payload/pallas_call | solution.py:295
  1.6 5.1 %collective-permute-start.2 = (bf16[40,2048]{1,0:T(8,128)(2,1)S(1)}, bf16[40,2048]{1,0:T(8,128)(2,1)S(1)}, u32[]{:S(2)}, u32[]{:S(2)}) collective-permute-start(bf16[40,2048]{1,0:T(8,128)(2,1)S(1)} %payload.1.rest_0_), channel_id=1, source_target_pairs={{0,6},{2,0},{4,2},{6,4},{1,7},{3,1},{5,3},{7,5},{8,14},{10,8},{12,... | collective-permute-start | bytes 491528 | tf_op jit(solution)/shard_map/ppermute | solution.py:310
  6.7 0.0 collective-permute-start.1
  6.7 1.0 %collective-permute-start = (bf16[40,2048]{1,0:T(8,128)(2,1)S(1)}, bf16[40,2048]{1,0:T(8,128)(2,1)S(1)}, u32[]{:S(2)}, u32[]{:S(2)}) collective-permute-start(bf16[40,2048]{1,0:T(8,128)(2,1)S(1)} %payload.1.rest_0_), channel_id=1, source_target_pairs={{0,2},{2,4},{4,6},{6,0},{1,3},{3,5},{5,7},{7,1},{8,10},{10,12},{12... | collective-permute-start | bytes 491528 | tf_op jit(solution)/shard_map/ppermute | solution.py:310
  7.7 6.8 %project.1 = bf16[4,2,3,16,128]{4,3,2,1,0:T(8,128)(2,1)S(1)} custom-call(s32[3]{0:T(128)} %counts_ref.1, bf16[384,5120]{1,0:T(8,128)(2,1)} %bitcast.22, bf16[384,5120]{1,0:T(8,128)(2,1)} %bitcast.23, bf16[128,5120]{1,0:T(8,128)(2,1)} %bitcast.24, bf16[5120,128]{1,0:T(8,128)(2,1)} %bitcast.25, bf16[64,5120]{1,0:T(8,128)(2,1)} %bitcast.26, ...), custom_call_target="tpu_custom_call" | custom-call | flops 1509949440 | bytes 11796480 | tf_op jit(solution)/shard_map/project/pallas_call | solution.py:180
  14.5 8.7 %all_to_all.10 = bf16[8,3,16,128]{3,2,1,0:T(8,128)(2,1)S(1)} all-to-all(bf16[8,3,16,128]{3,2,1,0:T(8,128)(2,1)S(1)} %bitcast.18), channel_id=1, replica_groups=mesh['feat'=4,'hi'=2,'lo'=2,'core'=2] {'feat','core'}, dimensions={0} | all-to-all | bytes 196608 | tf_op jit(solution)/shard_map/all_to_all | solution.py:328
  23.2 0.0 collective-permute-done.2.rest_3_
  23.2 0.0 collective-permute-done.1.rest_2_
  23.3 0.0 collective-permute-done.rest_1_
  23.3 0.9 %combine.1 = (bf16[3,2048]{1,0:T(4,128)(2,1)}, f32[4,2,8,128]{3,2,1,0:T(8,128)S(1)}) custom-call(s32[1]{0:T(128)} %bitcast.10.index_ref, bf16[4,2,3,16,128]{4,3,2,1,0:T(8,128)(2,1)S(1)} %bitcast.19, bf16[40,2048]{1,0:T(8,128)(2,1)S(1)} %payload.1.rest_0_, bf16[40,2048]{1,0:T(8,128)(2,1)S(1)} %collective-permute-done.rest_1_, ...), custom_call_target="tpu_custom_call" | custom-call | tf_op jit(solution)/shard_map/combine/pallas_call | solution.py:336
  24.2 7.2 %all_to_all.11 = f32[8,8,128]{2,1,0:T(8,128)S(1)} all-to-all(f32[8,8,128]{2,1,0:T(8,128)S(1)} %bitcast.21), channel_id=1, replica_groups=mesh['feat'=4,'hi'=2,'lo'=2,'core'=2] {'feat','core'}, dimensions={0} | all-to-all | bytes 65536 | tf_op jit(solution)/shard_map/all_to_all | solution.py:352
  31.4 0.7 %score.1 = f32[3,8]{1,0:T(4,128)} custom-call(f32[4,2,8,128]{3,2,1,0:T(8,128)S(1)} %bitcast.20), custom_call_target="tpu_custom_call" | custom-call | tf_op jit(solution)/shard_map/score/pallas_call | solution.py:353
Async XLA Ops:
  1.6 21.7 %collective-permute-start.2 = (bf16[40,2048]{1,0:T(8,128)(2,1)S(1)}, bf16[40,2048]{1,0:T(8,128)(2,1)S(1)}, u32[]{:S(2)}, u32[]{:S(2)}) collective-permute-start(bf16[40,2048]{1,0:T(8,128)(2,1)S(1)} %payload.1.rest_0_), channel_id=1, source_target_pairs={{0,6},{2,0},{4,2},{6,4},{1,7},{3,1},{5,3},{7,5},{8,14},{10,8},{12,... | collective-permute-start | bytes 491528 | tf_op jit(solution)/shard_map/ppermute | solution.py:310
  6.7 16.5 %collective-permute-start.1 = (bf16[40,2048]{1,0:T(8,128)(2,1)S(1)}, bf16[40,2048]{1,0:T(8,128)(2,1)S(1)}, u32[]{:S(2)}, u32[]{:S(2)}) collective-permute-start(bf16[40,2048]{1,0:T(8,128)(2,1)S(1)} %payload.1.rest_0_), channel_id=1, source_target_pairs={{0,4},{2,6},{4,0},{6,2},{1,5},{3,7},{5,1},{7,3},{8,12},{10,14},{12... | collective-permute-start | bytes 491528 | tf_op jit(solution)/shard_map/ppermute | solution.py:310
  6.7 16.5 %collective-permute-start = (bf16[40,2048]{1,0:T(8,128)(2,1)S(1)}, bf16[40,2048]{1,0:T(8,128)(2,1)S(1)}, u32[]{:S(2)}, u32[]{:S(2)}) collective-permute-start(bf16[40,2048]{1,0:T(8,128)(2,1)S(1)} %payload.1.rest_0_), channel_id=1, source_target_pairs={{0,2},{2,4},{4,6},{6,0},{1,3},{3,5},{5,7},{7,1},{8,10},{10,12},{12... | collective-permute-start | bytes 491528 | tf_op jit(solution)/shard_map/ppermute | solution.py:310

commit v5 on v4

--- a/solution.py
+++ b/solution.py
@@ -13,8 +13,8 @@
 DOMAINS = 8
 LANES = 128
 SUBLANES = 8
-CHUNKS = 4
-PROJECT_VMEM = 67_043_328 - 1_300_000
+CHUNKS = 2
+PROJECT_VMEM = 24 << 20
 
 FAR = ("hi", "lo")
 NEAR = ("core",)
@@ -62,8 +62,8 @@
     counts_ref,
     x_hbm,
     g_hbm,
-    a_hbm,
-    b_hbm,
+    a_ref,
+    b_ref,
     of_hbm,
     if_hbm,
     rb_hbm,
@@ -71,13 +71,13 @@
     out_ref,
     x_ref,
     g_ref,
-    wx_ref,
-    b_ref,
     of_ref,
+    if_ref,
     rb_ref,
     ra_ref,
     acc_x,
     acc_g,
+    rank_ref,
     x_sems,
     g_sems,
     sems,
@@ -85,23 +85,24 @@
     feat_size, copies, examples, part, _ = out_ref.shape
     chunks, tokens, chunk = x_ref.shape
     seq = tokens // examples
-    rank = a_hbm.shape[0]
+    rank = a_ref.shape[0]
     rows = of_hbm.shape[0]
 
+    def span_of(c):
+        return pl.ds(pl.multiple_of(c * chunk, LANES), chunk)
+
     def x_moves(c):
-        span = pl.ds(pl.multiple_of(c * chunk, LANES), chunk)
+        span = span_of(c)
         return (
             pltpu.make_async_copy(x_hbm.at[:, span], x_ref.at[c], x_sems.at[c, 0]),
-            pltpu.make_async_copy(a_hbm.at[:, span], wx_ref.at[c, :rank], x_sems.at[c, 1]),
-            pltpu.make_async_copy(if_hbm.at[:, span], wx_ref.at[c, rank:], x_sems.at[c, 2]),
+            pltpu.make_async_copy(if_hbm.at[:, span], if_ref.at[c], x_sems.at[c, 1]),
         )
 
     def g_moves(c):
-        span = pl.ds(pl.multiple_of(c * chunk, LANES), chunk)
+        span = span_of(c)
         return (
             pltpu.make_async_copy(g_hbm.at[:, span], g_ref.at[c], g_sems.at[c, 0]),
-            pltpu.make_async_copy(b_hbm.at[span, :], b_ref.at[c], g_sems.at[c, 1]),
-            pltpu.make_async_copy(of_hbm.at[:, span], of_ref.at[c], g_sems.at[c, 2]),
+            pltpu.make_async_copy(of_hbm.at[:, span], of_ref.at[c], g_sems.at[c, 1]),
         )
 
     small = [
@@ -129,31 +130,30 @@
     def _(c):
         for move in x_moves(c):
             move.wait()
-        acc_x[...] += dot32(x_ref[c], wx_ref[c], NT)
+        weights = jnp.concatenate([a_ref[:, span_of(c)], if_ref[c]], axis=0)
+        acc_x[...] += dot32(x_ref[c], weights, NT)
 
     for move in small:
         move.wait()
+    place = lax.broadcasted_iota(jnp.int32, (seq, rows), 0)
+    spans = [slice(e * seq, (e + 1) * seq) for e in range(examples)]
+    live = [place < counts_ref[e] for e in range(examples)]
+    hidden = acc_x[:, :rank].astype(jnp.bfloat16)
+    rank_ref[...] = dot32(hidden, rb_ref[...], NN).astype(jnp.bfloat16)
 
     @pl.loop(0, chunks)
     def _(c):
         for move in g_moves(c):
             move.wait()
-        weights = jnp.concatenate([b_ref[c], of_ref[c].T], axis=1)
+        weights = jnp.concatenate([b_ref[span_of(c), :], of_ref[c].T], axis=1)
         acc_g[...] += dot32(g_ref[c], weights, NN)
 
-    place = lax.broadcasted_iota(jnp.int32, (seq, rows), 0)
-
-    @pl.loop(0, examples)
-    def _(e):
-        span = pl.ds(pl.multiple_of(e * seq, seq), seq)
-        live = place < counts_ref[e]
-        hidden = acc_x[span, :rank].astype(jnp.bfloat16)
-        back = acc_g[span, :rank].astype(jnp.bfloat16)
-        hidden_rank = dot32(hidden, rb_ref[...], NN).astype(jnp.bfloat16)
-        back_rank = dot32(back, ra_ref[...], NN).astype(jnp.bfloat16)
-        gp = jnp.where(live, acc_g[span, rank:], 0.0).astype(jnp.bfloat16)
-        ip = jnp.where(live, acc_x[span, rank:], 0.0).astype(jnp.bfloat16)
-        term = dot32(gp, hidden_rank, TN) + dot32(ip, back_rank, TN)
+    back = acc_g[:, :rank].astype(jnp.bfloat16)
+    back_rank = dot32(back, ra_ref[...], NN).astype(jnp.bfloat16)
+    for e, span in enumerate(spans):
+        gp = jnp.where(live[e], acc_g[span, rank:], 0.0).astype(jnp.bfloat16)
+        ip = jnp.where(live[e], acc_x[span, rank:], 0.0).astype(jnp.bfloat16)
+        term = dot32(gp, rank_ref[span, :], TN) + dot32(ip, back_rank[span], TN)
         term = (term / counts_ref[e].astype(jnp.float32)).astype(jnp.bfloat16)
         for f in range(feat_size):
             for q in range(copies):
@@ -168,26 +168,30 @@
     out = (feat_size, copies, examples, rows // feat_size, rb.shape[1])
     hbm = pl.BlockSpec(memory_space=pltpu.HBM)
     vmem = pl.BlockSpec(memory_space=pltpu.VMEM)
+    fixed = [
+        pltpu.with_memory_space_constraint(array, pltpu.HBM) if n not in (2, 3) else array
+        for n, array in enumerate(arrays)
+    ]
     low = [
         (CHUNKS, tokens, chunk),
         (CHUNKS, tokens, chunk),
-        (CHUNKS, rank + rows, chunk),
-        (CHUNKS, chunk, rank),
+        (CHUNKS, rows, chunk),
         (CHUNKS, rows, chunk),
         rb.shape,
         rb.shape,
     ]
     return pl.pallas_call(
         project_kernel,
-        in_specs=[pl.BlockSpec(memory_space=pltpu.SMEM)] + [hbm] * len(arrays),
+        in_specs=[pl.BlockSpec(memory_space=pltpu.SMEM)] + [hbm] * 2 + [vmem] * 2 + [hbm] * 4,
         out_specs=vmem,
         out_shape=pltpu.VMEM(out, jnp.bfloat16),
         scratch_shapes=[pltpu.VMEM(shape, jnp.bfloat16) for shape in low]
         + [
             pltpu.VMEM((tokens, rank + rows), jnp.float32),
             pltpu.VMEM((tokens, rank + rows), jnp.float32),
-            pltpu.SemaphoreType.DMA((CHUNKS, 3)),
-            pltpu.SemaphoreType.DMA((CHUNKS, 3)),
+            pltpu.VMEM((tokens, rb.shape[1]), jnp.bfloat16),
+            pltpu.SemaphoreType.DMA((CHUNKS, 2)),
+            pltpu.SemaphoreType.DMA((CHUNKS, 2)),
             pltpu.SemaphoreType.DMA((2,)),
         ],
         cost_estimate=pl.CostEstimate(
@@ -197,7 +201,7 @@
         ),
         compiler_params=pltpu.CompilerParams(vmem_limit_bytes=PROJECT_VMEM),
         name="project",
-    )(counts, *arrays)
+    )(counts, *fixed)
 
 
 def combine_kernel(rows, index_ref, parts_ref, *rest):
@@ -301,9 +305,15 @@
             pltpu.VMEM((1, val_rows), jnp.int32),
             pltpu.SemaphoreType.DMA((2,)),
         ],
-        compiler_params=pltpu.CompilerParams(vmem_limit_bytes=PROJECT_VMEM),
+        cost_estimate=pl.CostEstimate(
+            flops=8_000_000_000, bytes_accessed=16_000_000, transcendentals=0
+        ),
+        compiler_params=limit(4),
         name="payload",
-    )(val_grads, val_domain.T)
+    )(
+        pltpu.with_memory_space_constraint(val_grads, pltpu.HBM),
+        pltpu.with_memory_space_constraint(val_domain.T, pltpu.HBM),
+    )
     pieces = [payload]
     for s in range(1, far_size):
         pairs = [(i, (i + s) % far_size) for i in range(far_size)]

time: 32.4 us -> 31.3 us (0.966)
  Pallas kernels: 9.42 us -> 8.32 us
    pallas_call x1, Pallas kernels: 6.81 us -> 5.56 us  [project(): pl.pallas_call(project_kernel, in_specs=[pl.BlockSpec(memory_space=pltpu....]
  transfers between devices with their start and end apart: 3 -> 3, of which waited for: 0 -> 0; matrix products, arithmetic and copies ran while one was open for 0% -> 0% of each run, Pallas kernels for 21% -> 18%
where the time goes in v5:
time: 31.3 us; the launch traced here: 31.1 us
  blocking collectives  15.9 us (51%)
  Pallas kernels  8.32 us (27%)
  starting transfers between devices  6.14 us (20%)
  between operations  0.68 us (2%)
    all_to_all x1, blocking collectives, local(): lax.all_to_all(flat_parts, group, 0, 0, tiled=True).reshape(parts.shape)  8.73 us
    all_to_all x1, blocking collectives, local(): lax.all_to_all(flat_packs, group, 0, 0, tiled=True).reshape(packs.shape)  7.2 us
    ppermute x3, starting transfers between devices, local(): pieces.append(lax.ppermute(payload, FAR, pairs))  6.14 us
    pallas_call x1, Pallas kernels, project(): pl.pallas_call(project_kernel, in_specs=[pl.BlockSpec(memory_space=pltpu....  5.56 us
    pallas_call x1, Pallas kernels, local(): pl.pallas_call(payload_kernel, in_specs=[pl.BlockSpec(memory_space=pltpu....  1.09 us
    pallas_call x1, Pallas kernels, local(): pl.pallas_call(functools.partial(combine_kernel, val_rows), in_specs=[sme...  0.92 us
    pallas_call x1, Pallas kernels, local(): pl.pallas_call(functools.partial(score_kernel, count, math.sqrt(PROJ)), o...  0.75 us
  transfers between devices with their start and end apart: 3, of which 0 were waited for; matrix products, arithmetic and copies ran while one was open for 0% of the time, Pallas kernels for 18%

profile of v5, /device:TPU:0, one launch (start us, length us, event | category | flops | bytes accessed | tf_op | source)
XLA Modules:
  0.0 31.1 jit_solution(2735687277954274104)
XLA Ops:
  0.6 0.0 copy-start
  0.6 0.0 copy-start.1
  0.7 0.0 copy-start.2
  0.7 1.1 %payload.1.rest_0_ = bf16[40,2048]{1,0:T(8,128)(2,1)S(1)} custom-call(bf16[32,2048]{1,0:T(8,128)(2,1)} %val_hbm.1, s32[1,32]{1,0:T(1,128)} %bitcast.30), custom_call_target="tpu_custom_call" | custom-call | flops 8000000000 | bytes 16000000 | tf_op jit(solution)/shard_map/payload/pallas_call | solution.py:299
  1.8 5.1 %collective-permute-start.2 = (bf16[40,2048]{1,0:T(8,128)(2,1)S(1)}, bf16[40,2048]{1,0:T(8,128)(2,1)S(1)}, u32[]{:S(2)}, u32[]{:S(2)}) collective-permute-start(bf16[40,2048]{1,0:T(8,128)(2,1)S(1)} %payload.1.rest_0_), channel_id=1, source_target_pairs={{0,6},{2,0},{4,2},{6,4},{1,7},{3,1},{5,3},{7,5},{8,14},{10,8},{12,... | collective-permute-start | bytes 491528 | tf_op jit(solution)/shard_map/ppermute | solution.py:320
  6.9 0.0 collective-permute-start.1
  6.9 1.0 %collective-permute-start = (bf16[40,2048]{1,0:T(8,128)(2,1)S(1)}, bf16[40,2048]{1,0:T(8,128)(2,1)S(1)}, u32[]{:S(2)}, u32[]{:S(2)}) collective-permute-start(bf16[40,2048]{1,0:T(8,128)(2,1)S(1)} %payload.1.rest_0_), channel_id=1, source_target_pairs={{0,2},{2,4},{4,6},{6,0},{1,3},{3,5},{5,7},{7,1},{8,10},{10,12},{12... | collective-permute-start | bytes 491528 | tf_op jit(solution)/shard_map/ppermute | solution.py:320
  7.9 0.0 copy-done
  7.9 0.0 copy-done.1
  7.9 0.0 copy-done.2
  7.9 5.6 %project.1 = bf16[4,2,3,16,128]{4,3,2,1,0:T(8,128)(2,1)S(1)} custom-call(s32[3]{0:T(128)S(1)} %copy-done.2, bf16[384,5120]{1,0:T(8,128)(2,1)} %bitcast.24, bf16[384,5120]{1,0:T(8,128)(2,1)} %bitcast.25, bf16[128,5120]{1,0:T(8,128)(2,1)S(1)} %bitcast.18, bf16[5120,128]{1,0:T(8,128)(2,1)S(1)} %bitcast.19, bf16[64,5120]{1,0:T(8,128)(2,1)} %bitcast.26, ...), custom_call_target="tpu_custom_call" | custom-call | flops 1509949440 | bytes 11796480 | tf_op jit(solution)/shard_map/project/pallas_call | solution.py:183
  13.5 8.7 %all_to_all.10 = bf16[8,3,16,128]{3,2,1,0:T(8,128)(2,1)S(1)} all-to-all(bf16[8,3,16,128]{3,2,1,0:T(8,128)(2,1)S(1)} %bitcast.20), channel_id=1, replica_groups=mesh['feat'=4,'hi'=2,'lo'=2,'core'=2] {'feat','core'}, dimensions={0} | all-to-all | bytes 196608 | tf_op jit(solution)/shard_map/all_to_all | solution.py:338
  22.2 0.0 collective-permute-done.2.rest_3_
  22.2 0.0 collective-permute-done.1.rest_2_
  22.2 0.0 collective-permute-done.rest_1_
  22.2 0.9 %combine.1 = (bf16[3,2048]{1,0:T(4,128)(2,1)}, f32[4,2,8,128]{3,2,1,0:T(8,128)S(1)}) custom-call(s32[1]{0:T(128)} %bitcast.10.index_ref, bf16[4,2,3,16,128]{4,3,2,1,0:T(8,128)(2,1)S(1)} %bitcast.21, bf16[40,2048]{1,0:T(8,128)(2,1)S(1)} %payload.1.rest_0_, bf16[40,2048]{1,0:T(8,128)(2,1)S(1)} %collective-permute-done.rest_1_, ...), custom_call_target="tpu_custom_call" | custom-call | tf_op jit(solution)/shard_map/combine/pallas_call | solution.py:346
  23.1 7.2 %all_to_all.11 = f32[8,8,128]{2,1,0:T(8,128)S(1)} all-to-all(f32[8,8,128]{2,1,0:T(8,128)S(1)} %bitcast.23), channel_id=1, replica_groups=mesh['feat'=4,'hi'=2,'lo'=2,'core'=2] {'feat','core'}, dimensions={0} | all-to-all | bytes 65536 | tf_op jit(solution)/shard_map/all_to_all | solution.py:362
  30.3 0.7 %score.1 = f32[3,8]{1,0:T(4,128)} custom-call(f32[4,2,8,128]{3,2,1,0:T(8,128)S(1)} %bitcast.22), custom_call_target="tpu_custom_call" | custom-call | tf_op jit(solution)/shard_map/score/pallas_call | solution.py:363
Async XLA Ops:
  0.6 7.3 %copy-start = (bf16[1,128,5120]{2,1,0:T(8,128)(2,1)S(1)}, bf16[1,128,5120]{2,1,0:T(8,128)(2,1)}, u32[]{:S(2)}) copy-start(bf16[1,128,5120]{2,1,0:T(8,128)(2,1)} %param.13) | copy-start | bytes 3932164
  0.6 7.3 %copy-start.1 = (bf16[1,5120,128]{2,1,0:T(8,128)(2,1)S(1)}, bf16[1,5120,128]{2,1,0:T(8,128)(2,1)}, u32[]{:S(2)}) copy-start(bf16[1,5120,128]{2,1,0:T(8,128)(2,1)} %param.14) | copy-start | bytes 3932164
  0.7 7.3 %copy-start.2 = (s32[3]{0:T(128)S(1)}, s32[3]{0:T(128)}, u32[]{:S(2)}) copy-start(s32[3]{0:T(128)} %counts_ref.1) | copy-start | bytes 40
  1.8 20.5 %collective-permute-start.2 = (bf16[40,2048]{1,0:T(8,128)(2,1)S(1)}, bf16[40,2048]{1,0:T(8,128)(2,1)S(1)}, u32[]{:S(2)}, u32[]{:S(2)}) collective-permute-start(bf16[40,2048]{1,0:T(8,128)(2,1)S(1)} %payload.1.rest_0_), channel_id=1, source_target_pairs={{0,6},{2,0},{4,2},{6,4},{1,7},{3,1},{5,3},{7,5},{8,14},{10,8},{12,... | collective-permute-start | bytes 491528 | tf_op jit(solution)/shard_map/ppermute | solution.py:320
  6.9 15.3 %collective-permute-start.1 = (bf16[40,2048]{1,0:T(8,128)(2,1)S(1)}, bf16[40,2048]{1,0:T(8,128)(2,1)S(1)}, u32[]{:S(2)}, u32[]{:S(2)}) collective-permute-start(bf16[40,2048]{1,0:T(8,128)(2,1)S(1)} %payload.1.rest_0_), channel_id=1, source_target_pairs={{0,4},{2,6},{4,0},{6,2},{1,5},{3,7},{5,1},{7,3},{8,12},{10,14},{12... | collective-permute-start | bytes 491528 | tf_op jit(solution)/shard_map/ppermute | solution.py:320
  6.9 15.3 %collective-permute-start = (bf16[40,2048]{1,0:T(8,128)(2,1)S(1)}, bf16[40,2048]{1,0:T(8,128)(2,1)S(1)}, u32[]{:S(2)}, u32[]{:S(2)}) collective-permute-start(bf16[40,2048]{1,0:T(8,128)(2,1)S(1)} %payload.1.rest_0_), channel_id=1, source_target_pairs={{0,2},{2,4},{4,6},{6,0},{1,3},{3,5},{5,7},{7,1},{8,10},{10,12},{12... | collective-permute-start | bytes 491528 | tf_op jit(solution)/shard_map/ppermute | solution.py:320
